TPU v7x, 32 devices: a whole 2x2x4 slice. The times are simulated.
32 devices in a mesh: leaf: 8 (over z, x), blk: 4 (over y, core).
Axes of the slice: x: 2, y: 2, z: 4, core: 2. Of those that a mesh axis runs over, the one named last changes fastest.
Arguments:
- desc_panel: bfloat16 [256, 384, 128], P(('leaf', 'blk')), may hold values from -18 to 18
- row_map: int32 [256, 3], P(('leaf', 'blk')), may hold values from 0 to 55, as said below
- anc_order: int32 [8], replicated, may hold values from 0 to 7, as said below
- anc_below: int32 [8, 12], replicated, may hold values from 32 to 55, as said below
- anc_panel: float32 [8, 4, 4, 128, 512], P('leaf', None, 'blk'), may hold values from -6 to 27, as said below
Outputs:
- chol_panel: float32 [8, 4, 4, 128, 512], P('leaf', None, 'blk')
Inputs may be any that keep to these rules, and one draw needn't show every extreme that they name: `row_map`: entry 0 of each row is a column block of one ancestor; the other entries are distinct entries of that ancestor's row of anc_below. Over the descendants of one device, entry 0 names the column blocks of any one ancestor at most 2 times, and of some ancestor exactly 2 times. `anc_order`: each leaf index holds a different column range. `anc_below`: each row holds 12 distinct indices. `anc_panel`: the leading 512 rows of each ancestor's panel are symmetric, and the leading block of S stays positive definite.
All inputs are finite; a program needn't handle non-finite values.
Results may differ from a plain program's by a relative error of at most 0.0003.
Values may be sent and summed in bfloat16 or wider, within the bound.
A program may use at most 192 MiB of HBM per device.

v0:
```python
import jax
import jax.numpy as jnp
from jax import lax
from jax.sharding import PartitionSpec as P

SLOTS = 2


slot_group = 16


def leaf_owner(ranges, anc_order):
    leaves = jnp.arange(anc_order.shape[0], dtype=jnp.int32)
    return jnp.sum(jnp.where(anc_order[None, :] == ranges[:, None], leaves[None, :], 0), axis=1)


def block_positions(block_ids, owner_leaf, anc_order, anc_below, column_blocks, position_count):
    column_base = anc_order[owner_leaf] * column_blocks
    relative = block_ids - column_base[:, None]
    in_columns = (relative >= 0) & (relative < column_blocks)
    below_ids = anc_below[owner_leaf]
    matching = block_ids[:, :, None] == below_ids[:, None, :]
    offsets = column_blocks + jnp.arange(below_ids.shape[1], dtype=jnp.int32)
    below_place = jnp.sum(jnp.where(matching, offsets[None, None, :], 0), axis=2)
    located = jnp.any(matching, axis=2)
    return jnp.where(in_columns, relative, jnp.where(located, below_place, position_count))


def place_blocks(running, group_place, group_products):
    return running + jnp.einsum(
        "kq,kxy->qxy", group_place, group_products, precision=lax.Precision.HIGHEST
    )


def shards(desc_panel, row_map, anc_order, anc_below, anc_panel):
    leaf_count = lax.axis_size("leaf")
    blk_count = lax.axis_size("blk")
    desc_count, block_count = row_map.shape
    block_rows = anc_panel.shape[3]
    panel_width = anc_panel.shape[4]
    wide_desc = desc_panel.shape[2]
    column_blocks = panel_width // block_rows
    position_count = column_blocks + anc_below.shape[1]
    slot_count = leaf_count * SLOTS
    group_count = slot_count // slot_group
    owner_leaf = leaf_owner(row_map[:, 0] // column_blocks, anc_order)
    positions = block_positions(
        row_map, owner_leaf, anc_order, anc_below, column_blocks, position_count
    )
    desc_index = jnp.arange(desc_count, dtype=jnp.int32)
    same_owner = owner_leaf[:, None] == owner_leaf[None, :]
    earlier = desc_index[None, :] < desc_index[:, None]
    ranking = jnp.sum(same_owner & earlier, axis=1)
    slot_of = owner_leaf * SLOTS + ranking
    matches = slot_of[None, :] == jnp.arange(slot_count, dtype=jnp.int32)[:, None]
    filled = jnp.any(matches, axis=1)
    chosen = jnp.sum(jnp.where(matches, desc_index[None, :], 0), axis=1)
    picked = jnp.where(filled, chosen, desc_count)
    slot_codes = jnp.where(filled[:, None], positions[chosen], position_count).reshape(
        leaf_count, SLOTS, block_count
    )
    send_rows = jnp.take(desc_panel, picked, axis=0, mode="fill", fill_value=0)
    send_rows = send_rows.reshape(leaf_count, SLOTS, block_count * block_rows, wide_desc)
    received, received_codes = (
        lax.all_to_all(send_rows, "leaf", split_axis=0, concat_axis=0, tiled=True),
        lax.all_to_all(
            slot_codes.astype(jnp.bfloat16), "leaf", split_axis=0, concat_axis=0, tiled=True
        ),
    )
    slot_data = received.reshape(group_count, slot_group, block_count * block_rows, wide_desc)

    def accumulate(running, element):
        group_data, group_place = element
        products = jnp.einsum(
            "kaw,kyw->kay",
            group_data,
            group_data[:, :block_rows],
            preferred_element_type=jnp.float32,
        )
        products = products.reshape(slot_group * block_count, block_rows, block_rows)
        return (place_blocks(running, group_place, products), None)

    codes_int = received_codes.astype(jnp.int32).reshape(slot_count, block_count)
    target = codes_int * column_blocks + codes_int[:, :1]
    placing = (
        target[:, :, None]
        == jnp.arange(position_count * column_blocks, dtype=jnp.int32)[None, None, :]
    ).astype(jnp.float32)
    placing = placing.reshape(group_count, slot_group * block_count, position_count * column_blocks)
    initial = jnp.zeros((position_count * column_blocks, block_rows, block_rows), jnp.float32)
    running, _ = lax.scan(accumulate, initial, (slot_data, placing))
    update = running.reshape(position_count, column_blocks, block_rows, block_rows).transpose(
        0, 2, 1, 3
    )
    update = update.reshape(position_count // blk_count, blk_count, block_rows, panel_width)
    local_rows = anc_panel[0]
    mine = lax.axis_index("blk")
    marker = (jnp.arange(blk_count, dtype=jnp.int32) == mine).astype(jnp.float32)
    combined = update - local_rows * marker[None, :, None, None]
    summed = lax.psum(combined, "blk")
    diagonal = -summed.reshape(position_count * block_rows, panel_width)[:panel_width]
    own_rows = -lax.dynamic_slice_in_dim(summed, mine, 1, 1)
    lower_factor = jnp.linalg.cholesky(diagonal)
    panel_rows = own_rows.reshape(-1, panel_width)
    solved = jax.scipy.linalg.solve_triangular(lower_factor, panel_rows.T, lower=True).T
    return solved.reshape(anc_panel.shape)


def solution(mesh):
    in_specs = (
        P(("leaf", "blk"), None, None),
        P(("leaf", "blk"), None),
        P(),
        P(),
        P("leaf", None, "blk", None, None),
    )
    out_specs = P("leaf", None, "blk", None, None)
    return jax.shard_map(shards, mesh=mesh, in_specs=in_specs, out_specs=out_specs, check_vma=False)
```

profile of v0, /device:TPU:0, one launch (start us, length us, event | category | flops | bytes accessed | tf_op | source)
XLA Modules:
  0.0 327.3 jit_solution(11401863305329569041)
XLA Ops:
  6.5 0.8 fusion.45
  7.3 0.8 select_reduce_fusion.5
  8.5 0.8 copy.53
  9.4 1.3 gather_fusion
  10.7 1.2 gather_fusion.1
  11.9 0.9 compare_reduce_fusion
  12.8 0.9 fusion.40
  14.8 0.7 copy.58
  15.5 7.3 %all-to-all-start = ((bf16[8,2,3]{2,1,0:T(2,128)(2,1)}), bf16[8,2,3]{2,1,0:T(2,128)(2,1)S(1)}, u32[]{:S(2)}, u32[]{:S(2)}) async-start(bf16[8,2,3]{2,1,0:T(2,128)(2,1)} %copy.58), calls=%async_computation | async-start | bytes 8192 | tf_op jit(solution)/shard_map/all_to_all | solution.py:66
  22.8 0.9 gather_fusion.3
  23.7 1.3 broadcast_select_fusion
  25.0 4.1 %all-to-all-done = bf16[8,2,3]{2,1,0:T(2,128)(2,1)S(1)} async-done(((bf16[8,2,3]{2,1,0:T(2,128)(2,1)}), bf16[8,2,3]{2,1,0:T(2,128)(2,1)S(1)}, u32[]{:S(2)}, u32[]{:S(2)}) %all-to-all-start) | async-done | bytes 128 | tf_op jit(solution)/shard_map/all_to_all | solution.py:66
  29.2 3.6 %all-to-all-start.1 = ((bf16[8,2,384,128]{3,2,1,0:T(8,128)(2,1)}), bf16[8,2,384,128]{3,2,1,0:T(8,128)(2,1)S(1)}, u32[]{:S(2)}, u32[]{:S(2)}) async-start(bf16[8,2,384,128]{3,2,1,0:T(8,128)(2,1)} %broadcast_select_fusion), calls=%async_computation.1 | async-start | bytes 3145728 | tf_op jit(solution)/shard_map/all_to_all | solution.py:65
  32.8 1.6 copy.62
  34.8 33.9 %all-to-all-done.1 = bf16[8,2,384,128]{3,2,1,0:T(8,128)(2,1)S(1)} async-done(((bf16[8,2,384,128]{3,2,1,0:T(8,128)(2,1)}), bf16[8,2,384,128]{3,2,1,0:T(8,128)(2,1)S(1)}, u32[]{:S(2)}, u32[]{:S(2)}) %all-to-all-start.1) | async-done | bytes 1572896 | tf_op jit(solution)/shard_map/all_to_all | solution.py:65
  69.3 6.0 %fusion.3 = f32[16,128,4,128]{3,0,1,2:T(8,128)} fusion(f32[48,128,128]{2,1,0:T(8,128)S(1)} %bitcast.107, s32[16,4]{0,1:T(4,128)S(1)} %multiply_add_fusion, s32[48]{0:T(128)S(1)} %add.130), kind=kOutput, calls=%fused_computation.10 | convolution fusion | flops 603982848 | bytes 7340480 | tf_op jit(solution)/shard_map/while/body/eval_jaxpr/kq,kxy->qxy/dot_general | solution.py:30
  75.3 5.4 %copy.61 = f32[16,128,4,128]{1,3,2,0:T(8,128)} copy(f32[16,128,4,128]{3,0,1,2:T(8,128)} %fusion.3) | data formatting | bytes 8388608 | tf_op jit(solution)/shard_map/transpose | solution.py:92
  80.7 4.7 %multiply_subtract_fusion = f32[4,4,128,512]{2,3,1,0:T(8,128)} fusion(f32[4,4,128,512]{2,3,1,0:T(8,128)} %bitcast.106, f32[4]{0:T(128)S(1)} %compare_convert_fusion, f32[4,128,512]{1,2,0:T(8,128)S(1)} %copy.62), kind=kLoop, calls=%fused_computation.6 | loop fusion | flops 2097152 | bytes 9437200 | tf_op jit(solution)/shard_map/sub | solution.py:99
  85.4 84.5 %all-reduce.3.cloned.1.call-done = f32[4,4,128,512]{2,3,1,0:T(8,128)} async-done(((f32[4,4,128,512]{2,3,1,0:T(8,128)}), f32[4,4,128,512]{2,3,1,0:T(8,128)}) %all-reduce.3.cloned.1.call-update) | async-done | bytes 4194320 | tf_op jit(solution)/shard_map/psum | solution.py:100
  169.8 1.3 slice_negate_fusion
  171.1 0.7 copy.63
  171.8 1.0 copy.84
  172.9 1.6 copy.64
  174.7 1.0 copy-done.2
  175.6 11.7 %cholesky.104 = f32[128,128]{1,0:T(8,128)S(1)} custom-call(f32[128,128]{1,0:T(8,128)S(1)} %cholesky.266), custom_call_target="Cholesky" | custom-call | tf_op jit(solution)/shard_map/jit(cholesky)/cholesky | solution.py:103
  187.5 9.8 %custom-call.31 = f32[1,128,128]{1,2,0:T(8,128)S(1)} custom-call(f32[1,128,128]{2,1,0:T(8,128)S(1)} %get-tuple-element.44), custom_call_target="InvertDiagBlocksLowerTriangular" | custom-call | tf_op jit(solution)/shard_map/jit(cholesky)/cholesky | solution.py:103
  197.3 1.2 constant_dynamic-update-slice_fusion.3
  198.6 1.3 convolution_subtract_fusion.3
  199.8 11.9 %cholesky.217 = f32[128,128]{1,0:T(8,128)S(1)} custom-call(f32[128,128]{1,0:T(8,128)S(1)} %cholesky.270), custom_call_target="Cholesky" | custom-call | tf_op jit(solution)/shard_map/jit(cholesky)/cholesky | solution.py:103
  211.8 0.7 compare_reduce_fusion.3
  213.1 9.8 %custom-call.32 = f32[1,128,128]{1,2,0:T(8,128)S(1)} custom-call(f32[1,128,128]{2,1,0:T(8,128)S(1)} %get-tuple-element.41), custom_call_target="InvertDiagBlocksLowerTriangular" | custom-call | tf_op jit(solution)/shard_map/jit(cholesky)/cholesky | solution.py:103
  223.2 1.3 convolution_subtract_fusion.4
  224.5 11.7 %cholesky.238 = f32[128,128]{1,0:T(8,128)S(1)} custom-call(f32[128,128]{1,0:T(8,128)S(1)} %cholesky.275), custom_call_target="Cholesky" | custom-call | tf_op jit(solution)/shard_map/jit(cholesky)/cholesky | solution.py:103
  236.2 0.7 compare_reduce_fusion.2
  236.9 9.8 %custom-call.33 = f32[1,128,128]{1,2,0:T(8,128)S(1)} custom-call(f32[1,128,128]{2,1,0:T(8,128)S(1)} %get-tuple-element.38), custom_call_target="InvertDiagBlocksLowerTriangular" | custom-call | tf_op jit(solution)/shard_map/jit(cholesky)/cholesky | solution.py:103
  247.0 1.2 convolution_subtract_fusion.5
  248.2 11.9 %cholesky.255 = f32[128,128]{1,0:T(8,128)S(1)} custom-call(f32[128,128]{1,0:T(8,128)S(1)} %convolution_subtract_fusion.5), custom_call_target="Cholesky" | custom-call | tf_op jit(solution)/shard_map/jit(cholesky)/cholesky | solution.py:103
  263.5 7.9 %while.1 = (s32[]{:T(128)}, f32[512,512]{1,0:T(8,128)S(1)}, s32[4,2]{0,1:T(2,128)S(1)}, f32[4,128,128]{2,1,0:T(8,128)S(1)}, s32[]{:T(128)}) while((s32[]{:T(128)}, f32[512,512]{1,0:T(8,128)S(1)}, s32[4,2]{0,1:T(2,128)S(1)}, f32[4,128,128]{2,1,0:T(8,128)S(1)}, s32[]{:T(128)}) %tuple.30), condition=%wide.while_cond, body=%wide.while_body.sunk | while | flops 2 | bytes 131181 | solution.py:105
  264.2 1.4 bitcast_dynamic-update-slice_fusion.2
  266.1 1.4 bitcast_dynamic-update-slice_fusion.2
  268.1 1.4 bitcast_dynamic-update-slice_fusion.2
  270.1 1.4 bitcast_dynamic-update-slice_fusion.2
  271.5 39.3 %custom-call.34 = f32[4,128,128]{1,2,0:T(8,128)S(1)} custom-call(f32[4,128,128]{2,1,0:T(8,128)S(1)} %get-tuple-element.24), custom_call_target="InvertDiagBlocksLowerTriangular" | custom-call | tf_op jit(solution)/shard_map/jit(_solve_triangular)/triangular_solve | solution.py:105
  310.8 1.3 dynamic-slice_negate_fusion
  313.2 1.2 convolution_subtract_fusion.1
  314.9 1.3 convolution_subtract_fusion
  316.6 1.6 convolution_subtract_fusion.2
  318.7 1.3 copy.72
  (69 shorter events, 9.8 us)
Async XLA Ops:
  6.5 16.3 %copy-start = (bf16[8,384,128]{2,1,0:T(8,128)(2,1)S(1)}, bf16[8,384,128]{2,1,0:T(8,128)(2,1)}, u32[]{:S(2)}) copy-start(bf16[8,384,128]{2,1,0:T(8,128)(2,1)} %param.5) | copy-start | bytes 2359300
  15.5 13.7 %all-to-all-start = ((bf16[8,2,3]{2,1,0:T(2,128)(2,1)}), bf16[8,2,3]{2,1,0:T(2,128)(2,1)S(1)}, u32[]{:S(2)}, u32[]{:S(2)}) async-start(bf16[8,2,3]{2,1,0:T(2,128)(2,1)} %copy.58), calls=%async_computation | async-start | bytes 8192 | tf_op jit(solution)/shard_map/all_to_all | solution.py:66
  29.2 39.5 %all-to-all-start.1 = ((bf16[8,2,384,128]{3,2,1,0:T(8,128)(2,1)}), bf16[8,2,384,128]{3,2,1,0:T(8,128)(2,1)S(1)}, u32[]{:S(2)}, u32[]{:S(2)}) async-start(bf16[8,2,384,128]{3,2,1,0:T(8,128)(2,1)} %broadcast_select_fusion), calls=%async_computation.1 | async-start | bytes 3145728 | tf_op jit(solution)/shard_map/all_to_all | solution.py:65
  32.7 137.1 %all-reduce.3.cloned.1.call-start = ((), (), s32[]{:S(2)}) async-start(), calls=%async_computation.2 | async-start | bytes 8388608 | tf_op jit(solution)/shard_map/psum | solution.py:100
  174.6 1.0 copy-start.2
  271.5 39.3 %copy-start.1 = (f32[512,512]{1,0:T(8,128)}, f32[512,512]{1,0:T(8,128)S(1)}, u32[]{:S(2)}) copy-start(f32[512,512]{1,0:T(8,128)S(1)} %get-tuple-element.101) | copy-start | bytes 3145732
Sparse Core Ops, SparseCore 0:
  85.5 84.3 all-reduce.2
where the time goes:
time: 333 us; the launch traced here: 327 us
  other arithmetic  132 us (40%)
  waiting for transfers between devices  123 us (37%)
  local copies, waits for them, and re-layouts  27.4 us (8%)
  matrix products  17.8 us (5%)
  between operations  16.8 us (5%)
  starting transfers between devices  10.9 us (3%)
    psum x1, waiting for transfers between devices, shards(): summed = lax.psum(combined, 'blk')  84.5 us
    another operation x15, other arithmetic, shards(): lower_factor = jnp.linalg.cholesky(diagonal)  79.5 us
    another operation x3, other arithmetic, shards(): jax.scipy.linalg.solve_triangular(lower_factor, panel_rows.T, lower=True)  39.4 us
    all_to_all x1, waiting for transfers between devices, shards(): lax.all_to_all(send_rows, 'leaf', split_axis=0, concat_axis=0, tiled=True)  33.9 us
    another operation x12, local copies, waits for them, and re-layouts  7.81 us
    all_to_all x1, starting transfers between devices, shards(): lax.all_to_all(slot_codes.astype(jnp.bfloat16), 'leaf', split_axis=0, con...  7.28 us
  transfers between devices with their start and end apart: 3, of which 3 were waited for; matrix products, arithmetic and copies ran while one was open for 1% of the time, Pallas kernels for 0%

commit v1 on v0

v1 whole, which is shorter than its diff:
```python
import jax
import jax.numpy as jnp
from jax import lax
from jax.experimental import pallas as pl
from jax.experimental.pallas import tpu as pltpu
from jax.sharding import PartitionSpec as P

SLOTS = 2

GROUP = 16


def split(x):
    hi = x.astype(jnp.bfloat16)
    return hi, (x - hi.astype(jnp.float32)).astype(jnp.bfloat16)


def dot_rows(lhs, rhs):
    lhs_hi, lhs_lo = lhs
    rhs_hi, rhs_lo = rhs
    return lax.dot_general(
        jnp.concatenate([lhs_hi, lhs_lo, lhs_hi], axis=0),
        jnp.concatenate([rhs_hi, rhs_hi, rhs_lo], axis=0),
        (((0,), (0,)), ((), ())),
        preferred_element_type=jnp.float32,
    )


def factor_strip(strip):
    tiles, rows, _ = strip.shape
    sub = lax.broadcasted_iota(jnp.int32, (GROUP, rows), 0)
    for g in range(rows // GROUP):
        r0 = g * GROUP
        held = [strip[q, r0 : r0 + GROUP, :] for q in range(tiles)]
        cols = [
            jnp.broadcast_to(held[0][:, r0 + t : r0 + t + 1], (GROUP, rows)) for t in range(GROUP)
        ]
        scale = jnp.zeros((GROUP, rows), jnp.float32)
        for t in range(GROUP):
            root = lax.rsqrt(cols[t][t : t + 1, :])
            scale = jnp.where(sub == t, root, scale)
            if t < GROUP - 1:
                mult = jnp.where(sub > t, cols[t], 0.0) * (root * root)
                for u in range(t + 1, GROUP):
                    cols[u] = cols[u] - mult * cols[u][t : t + 1, :]
                held = [h - mult * h[t : t + 1, :] for h in held]
        held = [h * scale for h in held]
        for q in range(tiles):
            strip[q, r0 : r0 + GROUP, :] = held[q]
        if r0 + GROUP < rows:
            pieces = [split(h) for h in held]
            rhs = tuple(jnp.concatenate([p[n] for p in pieces], axis=1) for n in range(2))
            drop = dot_rows(pieces[0], rhs)
            for q in range(tiles):
                strip[q, r0 + GROUP :, :] = (
                    strip[q, r0 + GROUP :, :] - drop[r0 + GROUP :, q * rows : (q + 1) * rows]
                )


def factor_kernel(top, own, other, upper, inverse, work, strip):
    blocks, rows = top.shape[0], top.shape[1]
    for j in range(blocks):
        for k in range(blocks):
            tile = top[j, :, k * rows : (k + 1) * rows]
            if j == k:
                tile = tile - own[k]
                for n in range(other.shape[0]):
                    tile = tile - other[n, k]
            work[j, k] = tile
    line = lax.broadcasted_iota(jnp.int32, (rows, rows), 0)
    lane = lax.broadcasted_iota(jnp.int32, (rows, rows), 1)

    def step(k, carry):
        strip[0] = work[k, k]
        strip[1] = jnp.where(line == lane, 1.0, 0.0)
        for q in range(1, blocks):
            strip[1 + q] = work[k, lax.rem(k + q, blocks)]
        factor_strip(strip)
        upper[k, k] = jnp.where(lane >= line, strip[0], 0.0)
        inverse[k, k] = strip[1]
        for q in range(1, blocks):
            j = lax.rem(k + q, blocks)
            ahead = k + q < blocks
            upper[k, j] = jnp.where(ahead, strip[1 + q], 0.0)
            inverse[k, j] = jnp.where(ahead, 0.0, strip[1 + q])
        pieces = [split(strip[1 + q]) for q in range(blocks)]
        rhs = tuple(jnp.concatenate([p[n] for p in pieces], axis=1) for n in range(2))
        for ahead in range(1, blocks):

            @pl.when(k + ahead < blocks)
            def _():
                j = k + ahead
                drop = dot_rows(split(strip[1 + ahead]), rhs)
                work[j, k] = -drop[:, :rows]
                for q in range(1, blocks):
                    at = lax.rem(k + q, blocks)
                    work[j, at] = work[j, at] - drop[:, q * rows : (q + 1) * rows]

        return carry

    lax.fori_loop(0, blocks, step, 0)


def factor(top, own, other):
    blocks, rows = top.shape[0], top.shape[1]
    square = jax.ShapeDtypeStruct((blocks, blocks, rows, rows), jnp.float32)
    return pl.pallas_call(
        factor_kernel,
        out_shape=(square, square),
        in_specs=[pl.BlockSpec(memory_space=pltpu.VMEM)] * 3,
        out_specs=(pl.BlockSpec(memory_space=pltpu.VMEM),) * 2,
        scratch_shapes=[
            pltpu.VMEM((blocks, blocks, rows, rows), jnp.float32),
            pltpu.VMEM((blocks + 1, rows, rows), jnp.float32),
        ],
        cost_estimate=pl.CostEstimate(
            flops=2 * (blocks * rows) ** 3, bytes_accessed=64 * 1024 * 1024, transcendentals=0
        ),
        name="factor",
    )(top, own, other)


def update_kernel(parity, codes, mine, theirs, diag, below):
    slots = mine.shape[0]
    rows = mine.shape[2]
    halves, per_dest, columns = below.shape[0], below.shape[1], below.shape[2]
    pair = 2
    blk_count = halves * pair
    position_count = (per_dest + 1) * blk_count
    block_count = mine.shape[1] // rows
    diag[...] = jnp.zeros_like(diag)
    below[...] = jnp.zeros_like(below)

    for half, source in enumerate((mine, theirs)):

        def absorb(s, carry, half=half, source=source):
            column = codes[half, s * block_count]

            @pl.when(column < position_count)
            def _():
                panel = source[s]
                product = lax.dot_general(
                    panel,
                    panel[:rows],
                    (((1,), (1,)), ((), ())),
                    preferred_element_type=jnp.float32,
                )
                diag[column] += product[:rows]
                for r in range(1, block_count):
                    place = codes[half, s * block_count + r]
                    dest = lax.rem(place, blk_count)

                    @pl.when((lax.rem(dest, pair) == parity[0]) & (place < position_count))
                    def _():
                        at = (lax.div(dest, pair), lax.div(place, blk_count) - 1, column)
                        below[at] += product[r * rows : (r + 1) * rows]

            return carry

        lax.fori_loop(0, slots, absorb, 0)


def local_update(parity, codes, mine, theirs, blk_count, columns, per_dest):
    rows = mine.shape[2]
    smem = pl.BlockSpec(memory_space=pltpu.SMEM)
    vmem = pl.BlockSpec(memory_space=pltpu.VMEM)
    return pl.pallas_call(
        update_kernel,
        out_shape=(
            jax.ShapeDtypeStruct((columns, rows, rows), jnp.float32),
            jax.ShapeDtypeStruct((blk_count // 2, per_dest, columns, rows, rows), jnp.float32),
        ),
        in_specs=[smem, smem, vmem, vmem],
        out_specs=(vmem, vmem),
        cost_estimate=pl.CostEstimate(
            flops=4 * mine.size * rows, bytes_accessed=8 * mine.size, transcendentals=0
        ),
        name="update",
    )(parity, codes, mine, theirs)


def finish_kernel(me, panel, own, other, upper, inverse, out):
    per_dest, rows = own.shape[0], own.shape[2]
    blocks = upper.shape[0]
    for k in range(blocks):
        tile = upper[k, me[0]]
        out[0, :, k * rows : (k + 1) * rows] = tile.T
    left = []
    for i in range(per_dest):
        parts = []
        for k in range(blocks):
            tile = panel[i + 1, :, k * rows : (k + 1) * rows] - own[i, k]
            for n in range(other.shape[0]):
                tile = tile - other[n, i, k]
            parts.append(tile)
        left.append(jnp.concatenate(parts, axis=1))
    whole_hi, whole_lo = split(jnp.concatenate(left, axis=0))
    for k in range(blocks):
        wide = (k + 1) * rows
        right = jnp.concatenate([inverse[k, q] for q in range(k + 1)], axis=1)
        right_hi, right_lo = split(right)

        def times(x, y):
            return lax.dot_general(
                x, y, (((1,), (1,)), ((), ())), preferred_element_type=jnp.float32
            )

        solved = (
            times(whole_hi[:, :wide], right_hi)
            + times(whole_lo[:, :wide], right_hi)
            + times(whole_hi[:, :wide], right_lo)
        )
        for i in range(per_dest):
            out[i + 1, :, k * rows : (k + 1) * rows] = solved[i * rows : (i + 1) * rows]


def finish(me, panel, own, other, upper, inverse):
    smem = pl.BlockSpec(memory_space=pltpu.SMEM)
    vmem = pl.BlockSpec(memory_space=pltpu.VMEM)
    return pl.pallas_call(
        finish_kernel,
        out_shape=jax.ShapeDtypeStruct(panel.shape, panel.dtype),
        in_specs=[smem] + [vmem] * 5,
        out_specs=vmem,
        cost_estimate=pl.CostEstimate(
            flops=6 * panel.size * panel.shape[2], bytes_accessed=8 * panel.size, transcendentals=0
        ),
        name="finish",
    )(me, panel, own, other, upper, inverse)


def leaf_owner(ranges, anc_order):
    leaves = jnp.arange(anc_order.shape[0], dtype=jnp.int32)
    return jnp.sum(jnp.where(anc_order[None, :] == ranges[:, None], leaves[None, :], 0), axis=1)


def block_positions(block_ids, owner_leaf, anc_order, anc_below, column_blocks, position_count):
    column_base = anc_order[owner_leaf] * column_blocks
    relative = block_ids - column_base[:, None]
    in_columns = (relative >= 0) & (relative < column_blocks)
    below_ids = anc_below[owner_leaf]
    matching = block_ids[:, :, None] == below_ids[:, None, :]
    offsets = column_blocks + jnp.arange(below_ids.shape[1], dtype=jnp.int32)
    below_place = jnp.sum(jnp.where(matching, offsets[None, None, :], 0), axis=2)
    located = jnp.any(matching, axis=2)
    return jnp.where(in_columns, relative, jnp.where(located, below_place, position_count))


def shards(desc_panel, row_map, anc_order, anc_below, anc_panel):
    leaf_count = lax.axis_size("leaf")
    blk_count = lax.axis_size("blk")
    desc_count, block_count = row_map.shape
    block_rows = anc_panel.shape[3]
    panel_width = anc_panel.shape[4]
    wide_desc = desc_panel.shape[2]
    column_blocks = panel_width // block_rows
    position_count = column_blocks + anc_below.shape[1]
    if column_blocks != blk_count or blk_count % 2 or wide_desc != block_rows:
        raise ValueError("unsupported sizes")
    slot_count = leaf_count * SLOTS
    mine = lax.axis_index("blk")
    swap = [(b, b ^ 1) for b in range(blk_count)]

    def shift(x, by):
        return lax.ppermute(x, "blk", [(b, (b + by) % blk_count) for b in range(blk_count)])

    local_rows = anc_panel.reshape(anc_panel.shape[1], block_rows, panel_width)
    own_top = local_rows[0]
    tops = [own_top] + [shift(own_top, by) for by in range(1, blk_count)]
    top = jnp.stack(tops)[(mine - jnp.arange(blk_count)) % blk_count]

    owner_leaf = leaf_owner(row_map[:, 0] // column_blocks, anc_order)
    positions = block_positions(
        row_map, owner_leaf, anc_order, anc_below, column_blocks, position_count
    )
    desc_index = jnp.arange(desc_count, dtype=jnp.int32)
    same_owner = owner_leaf[:, None] == owner_leaf[None, :]
    earlier = desc_index[None, :] < desc_index[:, None]
    ranking = jnp.sum(same_owner & earlier, axis=1)
    slot_of = owner_leaf * SLOTS + ranking
    matches = slot_of[None, :] == jnp.arange(slot_count, dtype=jnp.int32)[:, None]
    filled = jnp.any(matches, axis=1)
    chosen = jnp.sum(jnp.where(matches, desc_index[None, :], 0), axis=1)
    slot_codes = jnp.where(filled[:, None], positions[chosen], position_count).reshape(
        leaf_count, SLOTS * block_count
    )
    send_rows = jnp.take(desc_panel, chosen, axis=0)
    send_rows = send_rows.reshape(leaf_count, SLOTS, block_count * block_rows, wide_desc)
    received = lax.all_to_all(send_rows, "leaf", split_axis=0, concat_axis=0, tiled=True)
    codes = lax.all_to_all(
        slot_codes.astype(jnp.bfloat16), "leaf", split_axis=0, concat_axis=0, tiled=True
    )
    received = received.reshape(slot_count, block_count * block_rows, wide_desc)
    codes = codes.reshape(1, slot_count * block_count)
    their_rows = lax.ppermute(received, "blk", swap)
    their_codes = lax.ppermute(codes, "blk", swap)
    both_codes = jnp.concatenate([codes, their_codes], axis=0).astype(jnp.int32)

    per_dest = local_rows.shape[0] - 1
    parity = (mine % 2).astype(jnp.int32).reshape(1)
    diag, below = local_update(
        parity, both_codes, received, their_rows, blk_count, column_blocks, per_dest
    )
    half = blk_count // 2
    here = mine // 2
    steps = range(1, half)
    other_diag = jnp.stack([shift(diag, 2 * s) for s in steps])
    other_below = jnp.stack(
        [shift(lax.dynamic_index_in_dim(below, (here + s) % half, 0, False), 2 * s) for s in steps]
    )
    own_below = lax.dynamic_index_in_dim(below, here, 0, False)
    upper, inverse = factor(top, diag, other_diag)
    me = mine.astype(jnp.int32).reshape(1)
    out = finish(me, local_rows, own_below, other_below, upper, inverse)
    return out.reshape(anc_panel.shape)


def solution(mesh):
    in_specs = (
        P(("leaf", "blk"), None, None),
        P(("leaf", "blk"), None),
        P(),
        P(),
        P("leaf", None, "blk", None, None),
    )
    out_specs = P("leaf", None, "blk", None, None)
    return jax.shard_map(shards, mesh=mesh, in_specs=in_specs, out_specs=out_specs, check_vma=False)
```

time: 333 us -> 135 us (0.41); the launches traced: 327 us -> 133 us
  other arithmetic: 132 us -> 4.58 us
  waiting for transfers between devices: 123 us -> 74.8 us
  Pallas kernels: 0 us -> 30.1 us
  local copies, waits for them, and re-layouts: 27.4 us -> 9.19 us
  matrix products: 17.8 us -> 0 us
  between operations: 16.8 us -> 0.12 us
  starting transfers between devices: 10.9 us -> 14.7 us
    another operation x18 -> x1, other arithmetic: 119 us -> 0.07 us  [shards(): top = jnp.stack(tops)[(mine - jnp.arange(blk_count)) % blk_count]]
    psum x1 -> x0, waiting for transfers between devices: 84.5 us -> none  [shards(): summed = lax.psum(combined, 'blk')]
    ppermute x0 -> x7, waiting for transfers between devices: none -> 31.4 us  [the longest x5 30.3 us: shift(): lax.ppermute(x, 'blk', [(b, (b + by) % blk_count) for b in range(blk_coun...]
    pallas_call x0 -> x3, Pallas kernels: none -> 30.1 us  [the longest x1 19.3 us: factor(): pl.pallas_call(factor_kernel, out_shape=(square, square), in_specs=[pl.Bl...]
    another operation x13 -> x0, matrix products: 11.2 us -> none  [the longest x7 5.78 us: shards(): jax.scipy.linalg.solve_triangular(lower_factor, panel_rows.T, lower=True)]
    another operation x17 -> x0, local copies, waits for them, and re-layouts: 7.96 us -> none
    dot_general x2 -> x0, matrix products: 6.59 us -> none  [the longest x1 6.02 us: place_blocks(): jnp.einsum('kq,kxy->qxy', group_place, group_products, precision=lax.Prec...]
    transpose x1 -> x0, local copies, waits for them, and re-layouts: 5.37 us -> none  [shards(): running.reshape(position_count, column_blocks, block_rows, block_rows)]
  transfers between devices with their start and end apart: 3 -> 9, of which waited for: 3 -> 6; matrix products, arithmetic and copies ran while one was open for 1% -> 5% of each run, Pallas kernels for 0% -> 14%
where the time goes in v1:
time: 135 us; the launch traced here: 133 us
  waiting for transfers between devices  74.8 us (55%)
  Pallas kernels  30.1 us (22%)
  starting transfers between devices  14.7 us (11%)
  local copies, waits for them, and re-layouts  9.19 us (7%)
  other arithmetic  4.58 us (3%)
    all_to_all x1, waiting for transfers between devices, shards(): lax.all_to_all(send_rows, 'leaf', split_axis=0, concat_axis=0, tiled=True)  36.9 us
    ppermute x5, waiting for transfers between devices, shift(): lax.ppermute(x, 'blk', [(b, (b + by) % blk_count) for b in range(blk_coun...  30.3 us
    pallas_call x1, Pallas kernels, factor(): pl.pallas_call(factor_kernel, out_shape=(square, square), in_specs=[pl.Bl...  19.3 us
    all_to_all x1, starting transfers between devices, shards(): lax.all_to_all(send_rows, 'leaf', split_axis=0, concat_axis=0, tiled=True)  7.41 us
    pallas_call x1, Pallas kernels, local_update(): pl.pallas_call(update_kernel, out_shape=(jax.ShapeDtypeStruct((columns, r...  6.56 us
    all_to_all x1, waiting for transfers between devices, shards(): lax.all_to_all(slot_codes.astype(jnp.bfloat16), 'leaf', split_axis=0, con...  6.42 us
    pallas_call x1, Pallas kernels, finish(): pl.pallas_call(finish_kernel, out_shape=jax.ShapeDtypeStruct(panel.shape,...  4.25 us
    all_to_all x1, starting transfers between devices, shards(): lax.all_to_all(slot_codes.astype(jnp.bfloat16), 'leaf', split_axis=0, con...  3.65 us
  transfers between devices with their start and end apart: 9, of which 6 were waited for; matrix products, arithmetic and copies ran while one was open for 5% of the time, Pallas kernels for 14%

profile of v1, /device:TPU:0, one launch (start us, length us, event | category | flops | bytes accessed | tf_op | source)
XLA Modules:
  0.0 133.4 jit_solution(1423023090125263948)
XLA Ops:
  0.0 0.8 fusion.7
  0.8 0.8 select_reduce_fusion.1
  1.6 0.2 convert_reduce_fusion
  1.8 0.1 select_reduce_fusion
  1.9 0.1 reduce_sum.48
  2.0 0.9 gather_fusion.3
  2.9 1.4 %broadcast_select_fusion = bf16[8,2,384,128]{3,2,1,0:T(8,128)(2,1)} fusion(bf16[8,2,384,128]{3,2,1,0:T(8,128)(2,1)S(1)} %bitcast.37, pred[8,2]{1,0:T(8,128)(4,1)S(1)} %compare_and_fusion), kind=kLoop, calls=%fused_computation.5 | loop fusion | flops 786432 | bytes 3145744 | tf_op jit(solution)/shard_map/jit(_take)/select_n | solution.py:287
  4.2 7.4 %all-to-all-start.1 = ((bf16[8,2,384,128]{3,2,1,0:T(8,128)(2,1)}), bf16[8,2,384,128]{3,2,1,0:T(8,128)(2,1)S(1)}, u32[]{:S(2)}, u32[]{:S(2)}) async-start(bf16[8,2,384,128]{3,2,1,0:T(8,128)(2,1)} %broadcast_select_fusion), calls=%async_computation.1 | async-start | bytes 3145728 | tf_op jit(solution)/shard_map/all_to_all | solution.py:289
  11.7 0.1 copy.31
  11.7 36.9 %all-to-all-done.1 = bf16[8,2,384,128]{3,2,1,0:T(8,128)(2,1)S(1)} async-done(((bf16[8,2,384,128]{3,2,1,0:T(8,128)(2,1)}), bf16[8,2,384,128]{3,2,1,0:T(8,128)(2,1)S(1)}, u32[]{:S(2)}, u32[]{:S(2)}) %all-to-all-start.1) | async-done | bytes 1572896 | tf_op jit(solution)/shard_map/all_to_all | solution.py:289
  48.7 0.1 fusion.1
  48.8 0.1 broadcast_in_dim.90
  48.8 0.1 copy.30
  49.0 0.6 gather_fusion
  49.6 0.6 gather_fusion.1
  50.2 0.2 compare_reduce_fusion
  50.4 0.1 copy.32
  50.5 0.2 fusion
  50.7 0.1 copy.33
  50.8 0.1 select_select_fusion
  50.9 0.6 gather_fusion.2
  51.5 0.1 gather.23
  51.6 0.1 copy.34
  51.6 0.7 copy.35
  52.3 3.6 %all-to-all-start = ((bf16[8,1,6]{2,1,0:T(2,128)(2,1)}), bf16[8,1,6]{2,1,0:T(2,128)(2,1)S(1)}, u32[]{:S(2)}, u32[]{:S(2)}) async-start(bf16[8,1,6]{2,1,0:T(2,128)(2,1)} %copy.35), calls=%async_computation | async-start | bytes 8192 | tf_op jit(solution)/shard_map/all_to_all | solution.py:290
  56.0 6.4 %all-to-all-done = bf16[8,1,6]{2,1,0:T(2,128)(2,1)S(1)} async-done(((bf16[8,1,6]{2,1,0:T(2,128)(2,1)}), bf16[8,1,6]{2,1,0:T(2,128)(2,1)S(1)}, u32[]{:S(2)}, u32[]{:S(2)}) %all-to-all-start) | async-done | bytes 128 | tf_op jit(solution)/shard_map/all_to_all | solution.py:290
  62.4 0.1 reshape.154
  62.5 0.0 collective-permute-start
  62.5 1.1 collective-permute-done
  63.7 0.6 maximum_convert_fusion.codes
  64.3 0.0 collective-permute-done.1.theirs
  64.3 6.6 %update.1 = (f32[4,128,128]{2,1,0:T(8,128)}, f32[2,3,4,128,128]{4,3,2,1,0:T(8,128)}) custom-call(s32[1]{0:T(128)} %bitcast.2.parity, s32[2,48]{1,0:T(2,128)} %maximum_convert_fusion.codes, bf16[16,384,128]{2,1,0:T(8,128)(2,1)} %bitcast.36, bf16[16,384,128]{2,1,0:T(8,128)(2,1)} %collective-permute-done.1.theirs), custom_call_target="tpu_custom_call" | custom-call | flops 402653184 | bytes 6291456 | tf_op jit(solution)/shard_map/update/pallas_call | solution.py:167
  70.8 2.5 %dynamic-slice_bitcast_fusion = (f32[3,4,128,128]{3,2,1,0:T(8,128)S(1)}, f32[3,4,128,128]{3,2,1,0:T(8,128)}) fusion(f32[2,3,4,128,128]{4,3,2,1,0:T(8,128)} %get-tuple-element.9, s32[]{:T(128)S(6)} %select_n.132, s32[]{:T(128)S(6)} %select_n.130), kind=kLoop, calls=%fused_computation.7 | loop fusion | bytes 3145736 | tf_op jit(solution)/shard_map/jit(dynamic_index_in_dim)/squeeze | solution.py:309
  73.3 1.2 collective-permute-start.2
  74.4 1.0 slice_bitcast_fusion.1
  75.5 0.4 collective-permute-start.5
  75.9 1.1 collective-permute-start.4
  77.0 0.0 collective-permute-start.3
  77.0 0.9 collective-permute-start.6
  78.0 20.0 %collective-permute-done.5 = f32[128,512]{1,0:T(8,128)S(1)} collective-permute-done((f32[128,512]{1,0:T(8,128)S(1)}, f32[128,512]{1,0:T(8,128)S(1)}, u32[]{:S(2)}, u32[]{:S(2)}) %collective-permute-start.5) | collective-permute-done | bytes 262176 | tf_op jit(solution)/shard_map/ppermute | solution.py:265
  98.0 6.9 %collective-permute-done.4 = f32[128,512]{1,0:T(8,128)S(1)} collective-permute-done((f32[128,512]{1,0:T(8,128)S(1)}, f32[128,512]{1,0:T(8,128)S(1)}, u32[]{:S(2)}, u32[]{:S(2)}) %collective-permute-start.4) | collective-permute-done | bytes 262176 | tf_op jit(solution)/shard_map/ppermute | solution.py:265
  104.9 0.0 collective-permute-done.3
  104.9 0.1 pad_maximum_fusion
  105.0 1.6 %gather_fusion.4 = f32[4,128,512]{2,1,0:T(8,128)} fusion(f32[4,128,512]{2,1,0:T(8,128)S(1)} %pad_maximum_fusion, s32[1024]{0:T(1024)S(1)} %pad_clamp_fusion), kind=kCustom, calls=%fused_computation.4 | custom fusion | bytes 2097168 | tf_op jit(solution)/shard_map/gather | solution.py:270
  106.6 3.3 %collective-permute-done.6 = f32[4,128,128]{2,1,0:T(8,128)} collective-permute-done((f32[4,128,128]{2,1,0:T(8,128)S(1)}, f32[4,128,128]{2,1,0:T(8,128)}, u32[]{:S(2)}, u32[]{:S(2)}) %collective-permute-start.6) | collective-permute-done | bytes 262176 | tf_op jit(solution)/shard_map/ppermute | solution.py:265
  109.9 19.3 %factor.1 = (f32[4,4,128,128]{3,2,1,0:T(8,128)}, f32[4,4,128,128]{3,2,1,0:T(8,128)}) custom-call(f32[4,128,512]{2,1,0:T(8,128)} %gather_fusion.4, f32[4,128,128]{2,1,0:T(8,128)} %get-tuple-element.10.own, f32[1,4,128,128]{3,2,1,0:T(8,128)} %bitcast.19.other), custom_call_target="tpu_custom_call" | custom-call | flops 268435456 | bytes 67108864 | tf_op jit(solution)/shard_map/factor/pallas_call | solution.py:107
  129.2 0.0 collective-permute-done.2
  129.2 4.2 %finish.1 = f32[4,128,512]{2,1,0:T(8,128)} custom-call(s32[1]{0:T(128)} %bitcast.me, f32[4,128,512]{2,1,0:T(8,128)} %bitcast.38, f32[3,4,128,128]{3,2,1,0:T(8,128)} %get-tuple-element.14.own, f32[1,3,4,128,128]{4,3,2,1,0:T(8,128)} %bitcast.12.other, f32[4,4,128,128]{3,2,1,0:T(8,128)} %get-tuple-element.11.upper, f32[4,4,128,128]{3,2,1,0:T(8,128)} %get-tuple-element.12.inverse), custom_call_target="tpu_custom_call" | custom-call | flops 805306368 | bytes 2097152 | tf_op jit(solution)/shard_map/finish/pallas_call | solution.py:220
  (27 shorter events, 0.2 us)
Async XLA Ops:
  0.0 2.0 %copy-start = (bf16[8,384,128]{2,1,0:T(8,128)(2,1)S(1)}, bf16[8,384,128]{2,1,0:T(8,128)(2,1)}, u32[]{:S(2)}) copy-start(bf16[8,384,128]{2,1,0:T(8,128)(2,1)} %param.5) | copy-start | bytes 2359300
  4.2 7.4 %copy-start.5 = (s32[8,3]{0,1:T(4,128)S(1)}, s32[8,3]{0,1:T(4,128)}, u32[]{:S(2)}) copy-start(s32[8,3]{0,1:T(4,128)} %param.6) | copy-start | bytes 292
  4.2 44.8 %copy-start.1 = (s32[8]{0:T(128)S(1)}, s32[8]{0:T(128)}, u32[]{:S(2)}) copy-start(s32[8]{0:T(128)} %param.7) | copy-start | bytes 100
  4.2 45.4 %copy-start.3 = (s32[8,12]{1,0:T(8,128)S(1)}, s32[8,12]{1,0:T(8,128)}, u32[]{:S(2)}) copy-start(s32[8,12]{1,0:T(8,128)} %param.8) | copy-start | bytes 1156
  4.2 44.4 %all-to-all-start.1 = ((bf16[8,2,384,128]{3,2,1,0:T(8,128)(2,1)}), bf16[8,2,384,128]{3,2,1,0:T(8,128)(2,1)S(1)}, u32[]{:S(2)}, u32[]{:S(2)}) async-start(bf16[8,2,384,128]{3,2,1,0:T(8,128)(2,1)} %broadcast_select_fusion), calls=%async_computation.1 | async-start | bytes 3145728 | tf_op jit(solution)/shard_map/all_to_all | solution.py:289
  48.7 15.6 %copy-start.2 = (bf16[8,2,384,128]{3,2,1,0:T(8,128)(2,1)}, bf16[8,2,384,128]{3,2,1,0:T(8,128)(2,1)S(1)}, u32[]{:S(2)}) copy-start(bf16[8,2,384,128]{3,2,1,0:T(8,128)(2,1)S(1)} %all-to-all-done.1) | copy-start | bytes 4718596
  48.7 15.6 %collective-permute-start.1 = (bf16[16,384,128]{2,1,0:T(8,128)(2,1)S(1)}, bf16[16,384,128]{2,1,0:T(8,128)(2,1)}, u32[]{:S(2)}, u32[]{:S(2)}) collective-permute-start(bf16[16,384,128]{2,1,0:T(8,128)(2,1)S(1)} %bitcast.35), channel_id=1, source_target_pairs={{0,1},{1,0},{2,3},{3,2},{4,5},{5,4},{6,7},{7,6},{8,9},{9,8},{10,11... | collective-permute-start | bytes 4718600 | tf_op jit(solution)/shard_map/ppermute | solution.py:295
  52.3 10.1 %all-to-all-start = ((bf16[8,1,6]{2,1,0:T(2,128)(2,1)}), bf16[8,1,6]{2,1,0:T(2,128)(2,1)S(1)}, u32[]{:S(2)}, u32[]{:S(2)}) async-start(bf16[8,1,6]{2,1,0:T(2,128)(2,1)} %copy.35), calls=%async_computation | async-start | bytes 8192 | tf_op jit(solution)/shard_map/all_to_all | solution.py:290
  62.5 1.2 collective-permute-start
  70.8 6.2 %copy-start.4 = (f32[4,128,128]{2,1,0:T(8,128)S(1)}, f32[4,128,128]{2,1,0:T(8,128)}, u32[]{:S(2)}) copy-start(f32[4,128,128]{2,1,0:T(8,128)} %get-tuple-element.10.own) | copy-start | bytes 786436
  73.3 55.9 %collective-permute-start.2 = (f32[3,4,128,128]{3,2,1,0:T(8,128)S(1)}, f32[3,4,128,128]{3,2,1,0:T(8,128)}, u32[]{:S(2)}, u32[]{:S(2)}) collective-permute-start(f32[3,4,128,128]{3,2,1,0:T(8,128)S(1)} %get-tuple-element.13), channel_id=1, source_target_pairs={{0,2},{1,3},{2,0},{3,1},{4,6},{5,7},{6,4},{7,5},{8,10},{9,11},{10,... | collective-permute-start | bytes 2359304 | tf_op jit(solution)/shard_map/ppermute | solution.py:265
  75.5 22.5 %collective-permute-start.5 = (f32[128,512]{1,0:T(8,128)S(1)}, f32[128,512]{1,0:T(8,128)S(1)}, u32[]{:S(2)}, u32[]{:S(2)}) collective-permute-start(f32[128,512]{1,0:T(8,128)S(1)} %get-tuple-element.16), channel_id=1, source_target_pairs={{0,3},{1,0},{2,1},{3,2},{4,7},{5,4},{6,5},{7,6},{8,11},{9,8},{10,9... | collective-permute-start | bytes 786440 | tf_op jit(solution)/shard_map/ppermute | solution.py:265
  75.9 29.0 %collective-permute-start.4 = (f32[128,512]{1,0:T(8,128)S(1)}, f32[128,512]{1,0:T(8,128)S(1)}, u32[]{:S(2)}, u32[]{:S(2)}) collective-permute-start(f32[128,512]{1,0:T(8,128)S(1)} %get-tuple-element.16), channel_id=1, source_target_pairs={{0,2},{1,3},{2,0},{3,1},{4,6},{5,7},{6,4},{7,5},{8,10},{9,11},{10,... | collective-permute-start | bytes 786440 | tf_op jit(solution)/shard_map/ppermute | solution.py:265
  77.0 27.9 %collective-permute-start.3 = (f32[128,512]{1,0:T(8,128)S(1)}, f32[128,512]{1,0:T(8,128)S(1)}, u32[]{:S(2)}, u32[]{:S(2)}) collective-permute-start(f32[128,512]{1,0:T(8,128)S(1)} %get-tuple-element.16), channel_id=1, source_target_pairs={{0,1},{1,2},{2,3},{3,0},{4,5},{5,6},{6,7},{7,4},{8,9},{9,10},{10,1... | collective-permute-start | bytes 786440 | tf_op jit(solution)/shard_map/ppermute | solution.py:265
  77.0 32.8 %collective-permute-start.6 = (f32[4,128,128]{2,1,0:T(8,128)S(1)}, f32[4,128,128]{2,1,0:T(8,128)}, u32[]{:S(2)}, u32[]{:S(2)}) collective-permute-start(f32[4,128,128]{2,1,0:T(8,128)S(1)} %copy-done.4), channel_id=1, source_target_pairs={{0,2},{1,3},{2,0},{3,1},{4,6},{5,7},{6,4},{7,5},{8,10},{9,11},{10,... | collective-permute-start | bytes 786440 | tf_op jit(solution)/shard_map/ppermute | solution.py:265

commit v2 on v1

--- a/solution.py
+++ b/solution.py
@@ -6,6 +6,7 @@
 from jax.sharding import PartitionSpec as P
 
 SLOTS = 2
+PAIR = 2
 
 GROUP = 16
 
@@ -120,63 +121,204 @@
     )(top, own, other)
 
 
-def update_kernel(parity, codes, mine, theirs, diag, below):
-    slots = mine.shape[0]
-    rows = mine.shape[2]
-    halves, per_dest, columns = below.shape[0], below.shape[1], below.shape[2]
-    pair = 2
-    blk_count = halves * pair
+def update_kernel(me, codes, panels, diag, kept, sent):
+    leaves = codes.shape[1]
+    rows = panels.shape[2]
+    per_dest = kept.shape[0]
+    half = sent.shape[0] + 1
+    blk_count = half * PAIR
     position_count = (per_dest + 1) * blk_count
-    block_count = mine.shape[1] // rows
+    block_count = panels.shape[1] // rows
     diag[...] = jnp.zeros_like(diag)
-    below[...] = jnp.zeros_like(below)
-
-    for half, source in enumerate((mine, theirs)):
-
-        def absorb(s, carry, half=half, source=source):
-            column = codes[half, s * block_count]
-
-            @pl.when(column < position_count)
-            def _():
-                panel = source[s]
-                product = lax.dot_general(
-                    panel,
-                    panel[:rows],
-                    (((1,), (1,)), ((), ())),
-                    preferred_element_type=jnp.float32,
-                )
-                diag[column] += product[:rows]
-                for r in range(1, block_count):
-                    place = codes[half, s * block_count + r]
-                    dest = lax.rem(place, blk_count)
-
-                    @pl.when((lax.rem(dest, pair) == parity[0]) & (place < position_count))
-                    def _():
-                        at = (lax.div(dest, pair), lax.div(place, blk_count) - 1, column)
-                        below[at] += product[r * rows : (r + 1) * rows]
-
-            return carry
-
-        lax.fori_loop(0, slots, absorb, 0)
-
-
-def local_update(parity, codes, mine, theirs, blk_count, columns, per_dest):
-    rows = mine.shape[2]
+    kept[...] = jnp.zeros_like(kept)
+    sent[...] = jnp.zeros_like(sent)
+
+    def absorb(s, carry):
+        leaf = lax.div(s, SLOTS)
+        at = lax.rem(s, SLOTS) * block_count
+        column = codes[leaf, at]
+
+        @pl.when(column < position_count)
+        def _():
+            panel = panels[s]
+            product = lax.dot_general(
+                panel,
+                panel[:rows],
+                (((1,), (1,)), ((), ())),
+                preferred_element_type=jnp.float32,
+            )
+            diag[column] += product[:rows]
+            for r in range(1, block_count):
+                place = codes[leaf, at + r]
+                away = lax.rem(place, blk_count) + blk_count - me[0]
+                step = lax.rem(lax.div(away, PAIR), half)
+                index = lax.div(place, blk_count) - 1
+                inside = (lax.rem(away, PAIR) == 0) & (place < position_count)
+                block = product[r * rows : (r + 1) * rows]
+
+                @pl.when(inside & (step == 0))
+                def _():
+                    kept[index, column] += block
+
+                @pl.when(inside & (step > 0))
+                def _():
+                    sent[step - 1, index, column] += block
+
+        return carry
+
+    lax.fori_loop(0, panels.shape[0], absorb, 0)
+
+
+def local_update(me, codes, panels, blk_count, columns, per_dest):
+    rows = panels.shape[2]
     smem = pl.BlockSpec(memory_space=pltpu.SMEM)
     vmem = pl.BlockSpec(memory_space=pltpu.VMEM)
+    tiles = (per_dest, columns, rows, rows)
     return pl.pallas_call(
         update_kernel,
         out_shape=(
             jax.ShapeDtypeStruct((columns, rows, rows), jnp.float32),
-            jax.ShapeDtypeStruct((blk_count // 2, per_dest, columns, rows, rows), jnp.float32),
+            jax.ShapeDtypeStruct(tiles, jnp.float32),
+            jax.ShapeDtypeStruct((blk_count // PAIR - 1,) + tiles, jnp.float32),
         ),
-        in_specs=[smem, smem, vmem, vmem],
-        out_specs=(vmem, vmem),
+        in_specs=[smem, smem, vmem],
+        out_specs=(vmem, vmem, vmem),
         cost_estimate=pl.CostEstimate(
-            flops=4 * mine.size * rows, bytes_accessed=8 * mine.size, transcendentals=0
+            flops=2 * panels.size * rows, bytes_accessed=4 * panels.size, transcendentals=0
         ),
         name="update",
-    )(parity, codes, mine, theirs)
+    )(me, codes, panels)
+
+
+def exchange_kernel(rows_in, codes_in, top_in, rows_out, codes_out, tops_out, sems, top_sems, local):
+    leaves = rows_in.shape[0]
+    blks = tops_out.shape[0]
+    leaf = lax.axis_index("leaf")
+    blk = lax.axis_index("blk")
+    mate = blk + 1 - 2 * lax.rem(blk, PAIR)
+    MESH = pl.DeviceIdType.MESH
+
+    barrier = pltpu.get_barrier_semaphore()
+
+    def greet_leaf(s, carry):
+        pl.semaphore_signal(
+            barrier, inc=1, device_id=(lax.rem(leaf + s, leaves), blk), device_id_type=MESH
+        )
+        return carry
+
+    def greet_blk(s, carry):
+        pl.semaphore_signal(
+            barrier, inc=1, device_id=(leaf, lax.rem(blk + s, blks)), device_id_type=MESH
+        )
+        return carry
+
+    lax.fori_loop(1, leaves, greet_leaf, 0)
+    lax.fori_loop(1, blks, greet_blk, 0)
+    pl.semaphore_wait(barrier, leaves + blks - 2)
+
+    def remote(src, dst, kind, s, leaf_to, blk_to):
+        return pltpu.make_async_remote_copy(
+            src_ref=src,
+            dst_ref=dst,
+            send_sem=sems.at[kind, 0, s],
+            recv_sem=sems.at[kind, 1, s],
+            device_id=(leaf_to, blk_to),
+            device_id_type=MESH,
+        )
+
+    def outward(s):
+        to = lax.rem(leaf + s, leaves)
+        return (
+            remote(rows_in.at[to], rows_out.at[0, leaf], 0, s, to, blk),
+            remote(codes_in.at[to], codes_out.at[0, leaf], 1, s, to, blk),
+        )
+
+    def relay(s):
+        came = lax.rem(leaf + leaves - s, leaves)
+        return (
+            remote(rows_out.at[0, came], rows_out.at[1, came], 2, s, leaf, mate),
+            remote(codes_out.at[0, came], codes_out.at[1, came], 3, s, leaf, mate),
+        )
+
+    def relay_own():
+        return (
+            remote(rows_in.at[leaf], rows_out.at[1, leaf], 2, 0, leaf, mate),
+            remote(codes_in.at[leaf], codes_out.at[1, leaf], 3, 0, leaf, mate),
+        )
+
+    def top_copy(s):
+        return pltpu.make_async_remote_copy(
+            src_ref=top_in,
+            dst_ref=tops_out.at[blk],
+            send_sem=top_sems.at[0, s],
+            recv_sem=top_sems.at[1, s],
+            device_id=(leaf, lax.rem(blk + s, blks)),
+            device_id_type=MESH,
+        )
+
+    def start(s, carry):
+        for copy in outward(s):
+            copy.start()
+        return carry
+
+    lax.fori_loop(1, leaves, start, 0)
+    for s in range(1, blks):
+        top_copy(s).start()
+    for copy in relay_own():
+        copy.start()
+    kept = (
+        pltpu.make_async_copy(rows_in.at[leaf], rows_out.at[0, leaf], local.at[0]),
+        pltpu.make_async_copy(codes_in.at[leaf], codes_out.at[0, leaf], local.at[1]),
+        pltpu.make_async_copy(top_in, tops_out.at[blk], local.at[2]),
+    )
+    for copy in kept:
+        copy.start()
+
+    def forward(s, carry):
+        for copy in outward(s):
+            copy.wait_recv()
+        for copy in relay(s):
+            copy.start()
+        return carry
+
+    lax.fori_loop(1, leaves, forward, 0)
+    for copy in kept:
+        copy.wait()
+    for copy in relay_own():
+        copy.wait()
+    for s in range(1, blks):
+        top_copy(s).wait()
+
+    def drain(s, carry):
+        for copy in outward(s):
+            copy.wait_send()
+        for copy in relay(s):
+            copy.wait()
+        return carry
+
+    lax.fori_loop(1, leaves, drain, 0)
+
+
+def exchange(rows, codes, top, blk_count):
+    leaves = rows.shape[0]
+    vmem = pl.BlockSpec(memory_space=pltpu.VMEM)
+    return pl.pallas_call(
+        exchange_kernel,
+        out_shape=(
+            jax.ShapeDtypeStruct((PAIR,) + rows.shape, rows.dtype),
+            jax.ShapeDtypeStruct((PAIR,) + codes.shape, codes.dtype),
+            jax.ShapeDtypeStruct((blk_count,) + top.shape, top.dtype),
+        ),
+        in_specs=[vmem] * 3,
+        out_specs=(vmem,) * 3,
+        scratch_shapes=[
+            pltpu.SemaphoreType.DMA((4, 2, leaves)),
+            pltpu.SemaphoreType.DMA((2, blk_count)),
+            pltpu.SemaphoreType.DMA((3,)),
+        ],
+        compiler_params=pltpu.CompilerParams(collective_id=0, has_side_effects=True),
+        name="exchange",
+    )(rows, codes, top)
 
 
 def finish_kernel(me, panel, own, other, upper, inverse, out):
@@ -255,19 +397,12 @@
     wide_desc = desc_panel.shape[2]
     column_blocks = panel_width // block_rows
     position_count = column_blocks + anc_below.shape[1]
-    if column_blocks != blk_count or blk_count % 2 or wide_desc != block_rows:
+    if column_blocks != blk_count or blk_count % PAIR or wide_desc != block_rows:
         raise ValueError("unsupported sizes")
     slot_count = leaf_count * SLOTS
     mine = lax.axis_index("blk")
-    swap = [(b, b ^ 1) for b in range(blk_count)]
-
-    def shift(x, by):
-        return lax.ppermute(x, "blk", [(b, (b + by) % blk_count) for b in range(blk_count)])
-
+    me = mine.astype(jnp.int32).reshape(1)
     local_rows = anc_panel.reshape(anc_panel.shape[1], block_rows, panel_width)
-    own_top = local_rows[0]
-    tops = [own_top] + [shift(own_top, by) for by in range(1, blk_count)]
-    top = jnp.stack(tops)[(mine - jnp.arange(blk_count)) % blk_count]
 
     owner_leaf = leaf_owner(row_map[:, 0] // column_blocks, anc_order)
     positions = block_positions(
@@ -281,37 +416,27 @@
     matches = slot_of[None, :] == jnp.arange(slot_count, dtype=jnp.int32)[:, None]
     filled = jnp.any(matches, axis=1)
     chosen = jnp.sum(jnp.where(matches, desc_index[None, :], 0), axis=1)
-    slot_codes = jnp.where(filled[:, None], positions[chosen], position_count).reshape(
-        leaf_count, SLOTS * block_count
-    )
+    slot_codes = jnp.where(filled[:, None], positions[chosen], position_count)
+    slot_codes = slot_codes.reshape(leaf_count, 1, SLOTS * block_count)
+    slot_codes = jnp.pad(slot_codes, ((0, 0), (0, 0), (0, 128 - SLOTS * block_count)))
     send_rows = jnp.take(desc_panel, chosen, axis=0)
-    send_rows = send_rows.reshape(leaf_count, SLOTS, block_count * block_rows, wide_desc)
-    received = lax.all_to_all(send_rows, "leaf", split_axis=0, concat_axis=0, tiled=True)
-    codes = lax.all_to_all(
-        slot_codes.astype(jnp.bfloat16), "leaf", split_axis=0, concat_axis=0, tiled=True
-    )
-    received = received.reshape(slot_count, block_count * block_rows, wide_desc)
-    codes = codes.reshape(1, slot_count * block_count)
-    their_rows = lax.ppermute(received, "blk", swap)
-    their_codes = lax.ppermute(codes, "blk", swap)
-    both_codes = jnp.concatenate([codes, their_codes], axis=0).astype(jnp.int32)
+    send_rows = send_rows.reshape(leaf_count, SLOTS * block_count * block_rows, wide_desc)
+    panels, codes, top = exchange(send_rows, slot_codes.astype(jnp.int32), local_rows[0], blk_count)
+    panels = panels.reshape(PAIR * slot_count, block_count * block_rows, wide_desc)
+    codes = codes.reshape(PAIR * leaf_count, 128)
 
     per_dest = local_rows.shape[0] - 1
-    parity = (mine % 2).astype(jnp.int32).reshape(1)
-    diag, below = local_update(
-        parity, both_codes, received, their_rows, blk_count, column_blocks, per_dest
-    )
-    half = blk_count // 2
-    here = mine // 2
-    steps = range(1, half)
-    other_diag = jnp.stack([shift(diag, 2 * s) for s in steps])
-    other_below = jnp.stack(
-        [shift(lax.dynamic_index_in_dim(below, (here + s) % half, 0, False), 2 * s) for s in steps]
-    )
-    own_below = lax.dynamic_index_in_dim(below, here, 0, False)
+    diag, kept, sent = local_update(me, codes, panels, blk_count, column_blocks, per_dest)
+
+    def shift(x, by):
+        return lax.ppermute(x, "blk", [(b, (b + by) % blk_count) for b in range(blk_count)])
+
+    steps = range(1, blk_count // PAIR)
+    other_diag = jnp.stack([shift(diag, PAIR * s) for s in steps])
+    other_diag, sent = lax.optimization_barrier((other_diag, sent))
+    other_below = jnp.stack([shift(sent[s - 1], PAIR * s) for s in steps])
     upper, inverse = factor(top, diag, other_diag)
-    me = mine.astype(jnp.int32).reshape(1)
-    out = finish(me, local_rows, own_below, other_below, upper, inverse)
+    out = finish(me, local_rows, kept, other_below, upper, inverse)
     return out.reshape(anc_panel.shape)
 
 

time: 135 us -> 100 us (0.74)
  the two profiles are of different devices: /device:TPU:0 before, /device:TPU:10 now
where the time goes in v2:
time: 100 us
  Pallas kernels  74.6 us (75%)
  local copies, waits for them, and re-layouts  8.72 us (9%)
  waiting for transfers between devices  7.26 us (7%)
  other arithmetic  6.35 us (6%)
  starting transfers between devices  3.04 us (3%)
    pallas_call x1, Pallas kernels, exchange(): pl.pallas_call(exchange_kernel, out_shape=(jax.ShapeDtypeStruct((PAIR,) +...  43.6 us
    pallas_call x1, Pallas kernels, factor(): pl.pallas_call(factor_kernel, out_shape=(square, square), in_specs=[pl.Bl...  19.3 us
    pallas_call x1, Pallas kernels, local_update(): pl.pallas_call(update_kernel, out_shape=(jax.ShapeDtypeStruct((columns, r...  7.48 us
    ppermute x2, waiting for transfers between devices, shift(): lax.ppermute(x, 'blk', [(b, (b + by) % blk_count) for b in range(blk_coun...  7.26 us
    pallas_call x1, Pallas kernels, finish(): pl.pallas_call(finish_kernel, out_shape=jax.ShapeDtypeStruct(panel.shape,...  4.24 us
    ppermute x2, starting transfers between devices, shift(): lax.ppermute(x, 'blk', [(b, (b + by) % blk_count) for b in range(blk_coun...  3.04 us
    select_n x2, other arithmetic, shards(): send_rows = jnp.take(desc_panel, chosen, axis=0)  2.48 us
  transfers between devices with their start and end apart: 2, of which 1 were waited for; matrix products, arithmetic and copies ran while one was open for 0% of the time, Pallas kernels for 19%

profile of v2, /device:TPU:10, one launch (start us, length us, event | category | flops | bytes accessed | tf_op | source)
XLA Modules:
  0.0 100.1 jit_solution(4399179369351154546)
XLA Ops:
  0.0 0.0 copy-start
  0.0 0.8 fusion.5
  0.8 0.8 copy.22
  1.5 0.8 select_reduce_fusion.1
  2.4 0.2 convert_reduce_fusion
  2.6 0.1 select_reduce_fusion
  2.6 0.1 fusion.1
  2.7 0.1 reduce_sum.45
  2.8 1.3 %gather_fusion.1 = s32[8]{0:T(128)S(1)} fusion(s32[8]{0:T(128)} %param.7, s32[1024]{0:T(1024)S(1)} %pad_clamp_fusion), kind=kCustom, calls=%fused_computation.1 | custom fusion | bytes 96 | tf_op jit(solution)/shard_map/gather | solution.py:380
  4.1 1.2 %gather_fusion.2 = s32[8,12]{1,0:T(8,128)S(1)} fusion(s32[8,12]{1,0:T(8,128)} %param.8, s32[1024]{0:T(1024)S(1)} %pad_clamp_fusion), kind=kCustom, calls=%fused_computation.2 | custom fusion | bytes 800 | tf_op jit(solution)/shard_map/gather | solution.py:383
  5.4 0.9 compare_reduce_fusion
  6.3 0.9 fusion
  7.2 0.1 copy.24
  7.3 0.1 copy.23
  7.4 0.1 select_select_fusion
  7.4 0.6 gather_fusion.3
  8.0 0.1 gather.22
  8.1 0.1 broadcast_in_dim.99
  8.2 0.1 copy.21
  8.3 0.1 copy.25
  8.4 0.0 copy-done
  8.4 0.9 gather_fusion
  9.3 0.1 copy.20
  9.4 1.7 %slice_bitcast_fusion.top_in = f32[128,512]{1,0:T(8,128)} fusion(f32[1,4,1,128,512]{4,3,2,1,0:T(8,128)} %param.9), kind=kLoop, calls=%fused_computation.5 | loop fusion | bytes 524288 | tf_op jit(solution)/shard_map/squeeze | solution.py:424
  11.1 0.6 pad.4.codes_in
  11.7 0.1 broadcast_in_dim.95
  11.7 2.5 %bitcast_select_fusion.rows_in = bf16[8,768,128]{2,1,0:T(8,128)(2,1)} fusion(pred[8,768]{1,0:T(8,128)(4,1)S(1)} %bitcast.34, bf16[8,768,128]{2,1,0:T(8,128)(2,1)S(1)} %bitcast.29), kind=kLoop, calls=%fused_computation.4 | loop fusion | flops 786432 | bytes 3151872 | tf_op jit(solution)/shard_map/jit(_take)/select_n | solution.py:422
  14.2 43.6 %exchange.1 = (bf16[2,8,768,128]{3,2,1,0:T(8,128)(2,1)}, s32[2,8,1,128]{3,2,1,0:T(1,128)}, f32[4,128,512]{2,1,0:T(8,128)}) custom-call(bf16[8,768,128]{2,1,0:T(8,128)(2,1)} %bitcast_select_fusion.rows_in, s32[8,1,128]{2,1,0:T(1,128)} %pad.4.codes_in, f32[128,512]{1,0:T(8,128)} %slice_bitcast_fusion.top_in), custom_call_target="tpu_custom_call" | custom-call | tf_op jit(solution)/shard_map/exchange/pallas_call | solution.py:305
  57.8 7.5 %update.1 = (f32[4,128,128]{2,1,0:T(8,128)}, f32[3,4,128,128]{3,2,1,0:T(8,128)}, f32[1,3,4,128,128]{4,3,2,1,0:T(8,128)}) custom-call(s32[1]{0:T(128)} %bitcast.me, s32[16,128]{1,0:T(8,128)} %bitcast.36, bf16[32,384,128]{2,1,0:T(8,128)(2,1)} %bitcast.30), custom_call_target="tpu_custom_call" | custom-call | flops 402653184 | bytes 6291456 | tf_op jit(solution)/shard_map/update/pallas_call | solution.py:177
  65.3 1.5 %collective-permute-start = (f32[4,128,128]{2,1,0:T(8,128)}, f32[4,128,128]{2,1,0:T(8,128)S(1)}, u32[]{:S(2)}, u32[]{:S(2)}) collective-permute-start(f32[4,128,128]{2,1,0:T(8,128)} %get-tuple-element.18.own), channel_id=1, source_target_pairs={{0,2},{1,3},{2,0},{3,1},{4,6},{5,7},{6,4},{7,5},{8,10},{9,11},{10,... | collective-permute-start | bytes 786440 | tf_op jit(solution)/shard_map/ppermute | solution.py:432
  66.8 7.3 %collective-permute-done = f32[4,128,128]{2,1,0:T(8,128)S(1)} collective-permute-done((f32[4,128,128]{2,1,0:T(8,128)}, f32[4,128,128]{2,1,0:T(8,128)S(1)}, u32[]{:S(2)}, u32[]{:S(2)}) %collective-permute-start) | collective-permute-done | bytes 262176 | tf_op jit(solution)/shard_map/ppermute | solution.py:432
  74.1 0.0 copy-start.2
  74.1 1.5 %collective-permute-start.1 = (f32[3,4,128,128]{3,2,1,0:T(8,128)}, f32[3,4,128,128]{3,2,1,0:T(8,128)S(1)}, u32[]{:S(2)}, u32[]{:S(2)}) collective-permute-start(f32[3,4,128,128]{3,2,1,0:T(8,128)} %bitcast.37), channel_id=1, source_target_pairs={{0,2},{1,3},{2,0},{3,1},{4,6},{5,7},{6,4},{7,5},{8,10},{9,11},{10,... | collective-permute-start | bytes 2359304 | tf_op jit(solution)/shard_map/ppermute | solution.py:432
  75.6 0.0 copy-done.2
  75.6 19.3 %factor.1 = (f32[4,4,128,128]{3,2,1,0:T(8,128)}, f32[4,4,128,128]{3,2,1,0:T(8,128)}) custom-call(f32[4,128,512]{2,1,0:T(8,128)} %get-tuple-element.21.top, f32[4,128,128]{2,1,0:T(8,128)} %get-tuple-element.18.own, f32[1,4,128,128]{3,2,1,0:T(8,128)} %bitcast.33), custom_call_target="tpu_custom_call" | custom-call | flops 268435456 | bytes 67108864 | tf_op jit(solution)/shard_map/factor/pallas_call | solution.py:108
  94.9 0.0 collective-permute-done.1
  94.9 0.0 copy-start.1
  94.9 0.9 copy-done.1
  95.8 4.2 %finish.1 = f32[4,128,512]{2,1,0:T(8,128)} custom-call(s32[1]{0:T(128)} %bitcast.me, f32[4,128,512]{2,1,0:T(8,128)} %bitcast.31, f32[3,4,128,128]{3,2,1,0:T(8,128)} %get-tuple-element.17.own, f32[1,3,4,128,128]{4,3,2,1,0:T(8,128)} %bitcast.32, f32[4,4,128,128]{3,2,1,0:T(8,128)} %get-tuple-element.23.upper, f32[4,4,128,128]{3,2,1,0:T(8,128)} %get-tuple-element.24.inverse), custom_call_target="tpu_custom_call" | custom-call | flops 805306368 | bytes 2097152 | tf_op jit(solution)/shard_map/finish/pallas_call | solution.py:362
  (11 shorter events, 0.1 us)
Async XLA Ops:
  0.0 8.4 %copy-start = (bf16[8,384,128]{2,1,0:T(8,128)(2,1)S(1)}, bf16[8,384,128]{2,1,0:T(8,128)(2,1)}, u32[]{:S(2)}) copy-start(bf16[8,384,128]{2,1,0:T(8,128)(2,1)} %param.5) | copy-start | bytes 2359300
  65.3 8.8 %collective-permute-start = (f32[4,128,128]{2,1,0:T(8,128)}, f32[4,128,128]{2,1,0:T(8,128)S(1)}, u32[]{:S(2)}, u32[]{:S(2)}) collective-permute-start(f32[4,128,128]{2,1,0:T(8,128)} %get-tuple-element.18.own), channel_id=1, source_target_pairs={{0,2},{1,3},{2,0},{3,1},{4,6},{5,7},{6,4},{7,5},{8,10},{9,11},{10,... | collective-permute-start | bytes 786440 | tf_op jit(solution)/shard_map/ppermute | solution.py:432
  74.1 1.5 %copy-start.2 = (f32[4,128,128]{2,1,0:T(8,128)}, f32[4,128,128]{2,1,0:T(8,128)S(1)}, u32[]{:S(2)}) copy-start(f32[4,128,128]{2,1,0:T(8,128)S(1)} %collective-permute-done) | copy-start | bytes 786436
  74.1 20.8 %collective-permute-start.1 = (f32[3,4,128,128]{3,2,1,0:T(8,128)}, f32[3,4,128,128]{3,2,1,0:T(8,128)S(1)}, u32[]{:S(2)}, u32[]{:S(2)}) collective-permute-start(f32[3,4,128,128]{3,2,1,0:T(8,128)} %bitcast.37), channel_id=1, source_target_pairs={{0,2},{1,3},{2,0},{3,1},{4,6},{5,7},{6,4},{7,5},{8,10},{9,11},{10,... | collective-permute-start | bytes 2359304 | tf_op jit(solution)/shard_map/ppermute | solution.py:432
  94.9 0.9 copy-start.1

commit v3 on v2

v3 whole, which is shorter than its diff:
```python
import jax
import jax.numpy as jnp
from jax import lax
from jax.experimental import pallas as pl
from jax.experimental.pallas import tpu as pltpu
from jax.sharding import PartitionSpec as P

SLOTS = 2
PAIR = 2

GROUP = 16


def split(x):
    hi = x.astype(jnp.bfloat16)
    return hi, (x - hi.astype(jnp.float32)).astype(jnp.bfloat16)


def dot_rows(lhs, rhs):
    lhs_hi, lhs_lo = lhs
    rhs_hi, rhs_lo = rhs
    return lax.dot_general(
        jnp.concatenate([lhs_hi, lhs_lo, lhs_hi], axis=0),
        jnp.concatenate([rhs_hi, rhs_hi, rhs_lo], axis=0),
        (((0,), (0,)), ((), ())),
        preferred_element_type=jnp.float32,
    )


def factor_strip(strip):
    tiles, rows, _ = strip.shape
    sub = lax.broadcasted_iota(jnp.int32, (GROUP, rows), 0)
    for g in range(rows // GROUP):
        r0 = g * GROUP
        held = [strip[q, r0 : r0 + GROUP, :] for q in range(tiles)]
        cols = [
            jnp.broadcast_to(held[0][:, r0 + t : r0 + t + 1], (GROUP, rows)) for t in range(GROUP)
        ]
        scale = jnp.zeros((GROUP, rows), jnp.float32)
        for t in range(GROUP):
            root = lax.rsqrt(cols[t][t : t + 1, :])
            scale = jnp.where(sub == t, root, scale)
            if t < GROUP - 1:
                mult = jnp.where(sub > t, cols[t], 0.0) * (root * root)
                for u in range(t + 1, GROUP):
                    cols[u] = cols[u] - mult * cols[u][t : t + 1, :]
                held = [h - mult * h[t : t + 1, :] for h in held]
        held = [h * scale for h in held]
        for q in range(tiles):
            strip[q, r0 : r0 + GROUP, :] = held[q]
        if r0 + GROUP < rows:
            pieces = [split(h) for h in held]
            rhs = tuple(jnp.concatenate([p[n] for p in pieces], axis=1) for n in range(2))
            drop = dot_rows(pieces[0], rhs)
            for q in range(tiles):
                strip[q, r0 + GROUP :, :] = (
                    strip[q, r0 + GROUP :, :] - drop[r0 + GROUP :, q * rows : (q + 1) * rows]
                )


def factor_kernel(top, own, upper, inverse, work, strip):
    blocks, rows = top.shape[0], top.shape[1]
    for j in range(blocks):
        for k in range(blocks):
            tile = top[j, :, k * rows : (k + 1) * rows]
            if j == k:
                tile = tile - own[k]
            work[j, k] = tile
    line = lax.broadcasted_iota(jnp.int32, (rows, rows), 0)
    lane = lax.broadcasted_iota(jnp.int32, (rows, rows), 1)

    def step(k, carry):
        strip[0] = work[k, k]
        strip[1] = jnp.where(line == lane, 1.0, 0.0)
        for q in range(1, blocks):
            strip[1 + q] = work[k, lax.rem(k + q, blocks)]
        factor_strip(strip)
        upper[k, k] = jnp.where(lane >= line, strip[0], 0.0)
        inverse[k, k] = strip[1]
        for q in range(1, blocks):
            j = lax.rem(k + q, blocks)
            ahead = k + q < blocks
            upper[k, j] = jnp.where(ahead, strip[1 + q], 0.0)
            inverse[k, j] = jnp.where(ahead, 0.0, strip[1 + q])
        pieces = [split(strip[1 + q]) for q in range(blocks)]
        rhs = tuple(jnp.concatenate([p[n] for p in pieces], axis=1) for n in range(2))
        for ahead in range(1, blocks):

            @pl.when(k + ahead < blocks)
            def _():
                j = k + ahead
                drop = dot_rows(split(strip[1 + ahead]), rhs)
                work[j, k] = -drop[:, :rows]
                for q in range(1, blocks):
                    at = lax.rem(k + q, blocks)
                    work[j, at] = work[j, at] - drop[:, q * rows : (q + 1) * rows]

        return carry

    lax.fori_loop(0, blocks, step, 0)


def factor(top, own):
    blocks, rows = top.shape[0], top.shape[1]
    square = jax.ShapeDtypeStruct((blocks, blocks, rows, rows), jnp.float32)
    return pl.pallas_call(
        factor_kernel,
        out_shape=(square, square),
        in_specs=[pl.BlockSpec(memory_space=pltpu.VMEM)] * 2,
        out_specs=(pl.BlockSpec(memory_space=pltpu.VMEM),) * 2,
        scratch_shapes=[
            pltpu.VMEM((blocks, blocks, rows, rows), jnp.float32),
            pltpu.VMEM((blocks + 1, rows, rows), jnp.float32),
        ],
        cost_estimate=pl.CostEstimate(
            flops=2 * (blocks * rows) ** 3, bytes_accessed=64 * 1024 * 1024, transcendentals=0
        ),
        name="factor",
    )(top, own)


def pack_kernel(row_map, anc_order, anc_below, panels, heads, tails, codes, count):
    desc_count, block_count = row_map.shape
    leaves, below_count = anc_below.shape
    rows = heads.shape[2]
    columns = count.shape[0] // leaves
    position_count = columns + below_count
    heads[...] = jnp.zeros_like(heads)
    tails[...] = jnp.zeros_like(tails)

    def clear(leaf, carry):
        count[leaf] = 0
        for at in range(SLOTS * block_count):
            codes[leaf, at] = position_count
        return carry

    lax.fori_loop(0, leaves, clear, 0)

    def put(d, carry):
        head = row_map[d, 0]
        group = lax.div(head, columns)
        owner = lax.fori_loop(
            0,
            leaves,
            lambda leaf, best: jnp.where(anc_order[leaf] == group, leaf, best),
            0,
            unroll=leaves <= 16,
        )
        slot = count[owner]
        count[owner] = slot + 1
        at = slot * block_count
        codes[owner, at] = head - group * columns
        for r in range(1, block_count):
            block = row_map[d, r]
            place = position_count
            for q in range(below_count):
                place = jnp.where(anc_below[owner, q] == block, columns + q, place)
            codes[owner, at + r] = place
        heads[owner, slot] = panels[d, :rows]
        tails[owner, slot] = panels[d, rows:]
        return carry

    lax.fori_loop(0, desc_count, put, 0)


def pack(row_map, anc_order, anc_below, panels, columns, rows):
    leaves = anc_order.shape[0]
    wide = panels.shape[2]
    smem = pl.BlockSpec(memory_space=pltpu.SMEM)
    vmem = pl.BlockSpec(memory_space=pltpu.VMEM)
    return pl.pallas_call(
        pack_kernel,
        out_shape=(
            jax.ShapeDtypeStruct((leaves, SLOTS, rows, wide), panels.dtype),
            jax.ShapeDtypeStruct((leaves, SLOTS, panels.shape[1] - rows, wide), panels.dtype),
            jax.ShapeDtypeStruct((leaves, 128), jnp.int32),
        ),
        in_specs=[smem, smem, smem, vmem],
        out_specs=(vmem, vmem, smem),
        scratch_shapes=[pltpu.SMEM((leaves * columns,), jnp.int32)],
        name="pack",
    )(row_map, anc_order, anc_below, panels)


def update_kernel(me, codes, heads, tails, diag, kept):
    step = pl.program_id(0)
    leaves = heads.shape[0]
    rows = heads.shape[2]
    per_dest, columns = kept.shape[0], kept.shape[1]
    blk_count = columns
    position_count = (per_dest + 1) * blk_count
    block_count = 1 + tails.shape[2] // rows

    @pl.when(step == 0)
    def _():
        diag[...] = jnp.zeros_like(diag)
        kept[...] = jnp.zeros_like(kept)

    def absorb(s, carry):
        leaf = lax.div(s, SLOTS)
        slot = lax.rem(s, SLOTS)
        line = step * leaves + leaf
        at = slot * block_count
        column = codes[line, at]

        @pl.when(column < position_count)
        def _():
            head = heads[leaf, slot]

            def times(x):
                return lax.dot_general(
                    x, head, (((1,), (1,)), ((), ())), preferred_element_type=jnp.float32
                )

            diag[column] += times(head)
            for r in range(1, block_count):
                place = codes[line, at + r]
                index = lax.div(place, blk_count) - 1

                @pl.when((lax.rem(place, blk_count) == me[0]) & (place < position_count))
                def _():
                    kept[index, column] += times(tails[leaf, slot, (r - 1) * rows : r * rows])

        return carry

    lax.fori_loop(0, leaves * SLOTS, absorb, 0)


def local_update(me, codes, heads, tails, columns, per_dest):
    sources, leaves, slots, rows, wide = heads.shape
    smem = pl.BlockSpec(memory_space=pltpu.SMEM)
    chunk = min(leaves, 8)
    steps = sources * leaves // chunk
    heads = heads.reshape((steps, chunk) + heads.shape[2:])
    tails = tails.reshape((steps, chunk) + tails.shape[2:])
    out_shape = (
        jax.ShapeDtypeStruct((columns, rows, rows), jnp.float32),
        jax.ShapeDtypeStruct((per_dest, columns, rows, rows), jnp.float32),
    )
    return pl.pallas_call(
        update_kernel,
        grid=(steps,),
        out_shape=out_shape,
        in_specs=[
            smem,
            smem,
            pl.BlockSpec((None,) + heads.shape[1:], lambda i: (i, 0, 0, 0, 0)),
            pl.BlockSpec((None,) + tails.shape[1:], lambda i: (i, 0, 0, 0, 0)),
        ],
        out_specs=(
            pl.BlockSpec(out_shape[0].shape, lambda i: (0, 0, 0)),
            pl.BlockSpec(out_shape[1].shape, lambda i: (0, 0, 0, 0)),
        ),
        name="update",
    )(me, codes, heads, tails)


def exchange_kernel(
    heads_in, tails_in, codes_in, top_in, heads, tails, codes, tops, sems, top_sems, local
):
    leaves = heads_in.shape[0]
    blks = tops.shape[0]
    leaf = lax.axis_index("leaf")
    blk = lax.axis_index("blk")
    mate = blk + 1 - 2 * lax.rem(blk, PAIR)
    across = lax.rem(blk + PAIR, blks)
    MESH = pl.DeviceIdType.MESH
    loads = ((codes_in, codes), (heads_in, heads), (tails_in, tails))

    barrier = pltpu.get_barrier_semaphore()

    def greet_leaf(s, carry):
        pl.semaphore_signal(
            barrier, inc=1, device_id=(lax.rem(leaf + s, leaves), blk), device_id_type=MESH
        )
        return carry

    def greet_blk(s, carry):
        pl.semaphore_signal(
            barrier, inc=1, device_id=(leaf, lax.rem(blk + s, blks)), device_id_type=MESH
        )
        return carry

    lax.fori_loop(1, leaves, greet_leaf, 0)
    lax.fori_loop(1, blks, greet_blk, 0)
    pl.semaphore_wait(barrier, leaves + blks - 2)

    def remote(src, dst, load, kind, s, leaf_to, blk_to):
        return pltpu.make_async_remote_copy(
            src_ref=src,
            dst_ref=dst,
            send_sem=sems.at[load, kind, 0, s],
            recv_sem=sems.at[load, kind, 1, s],
            device_id=(leaf_to, blk_to),
            device_id_type=MESH,
        )

    def outward(load, s):
        source, held = loads[load]
        to = lax.rem(leaf + s, leaves)
        return remote(source.at[to], held.at[0, leaf], load, 0, s, to, blk)

    def came(s):
        return lax.rem(leaf + leaves - s, leaves)

    def to_mate(load, s):
        held = loads[load][1]
        return remote(held.at[0, came(s)], held.at[1, came(s)], load, 1, s, leaf, mate)

    def to_across(load, s):
        held = loads[load][1]
        return remote(held.at[0, came(s)], held.at[2, came(s)], load, 2, s, leaf, across)

    def passed_on(load, s):
        held = loads[load][1]
        return remote(held.at[2, came(s)], held.at[3, came(s)], load, 3, s, leaf, mate)

    def own(load):
        source, held = loads[load]
        return (
            remote(source.at[leaf], held.at[1, leaf], load, 1, 0, leaf, mate),
            remote(source.at[leaf], held.at[2, leaf], load, 2, 0, leaf, across),
        )

    def top_copy(s):
        return pltpu.make_async_remote_copy(
            src_ref=top_in,
            dst_ref=tops.at[blk],
            send_sem=top_sems.at[0, s],
            recv_sem=top_sems.at[1, s],
            device_id=(leaf, lax.rem(blk + s, blks)),
            device_id_type=MESH,
        )

    both = ((0, 1), (2,))

    def start(group):
        def one(s, carry):
            for load in group:
                outward(load, s).start()
            return carry

        lax.fori_loop(1, leaves, one, 0)

    start(both[0])
    kept = [
        pltpu.make_async_copy(source.at[leaf], held.at[0, leaf], local.at[load])
        for load, (source, held) in enumerate(loads)
    ]
    kept.append(pltpu.make_async_copy(top_in, tops.at[blk], local.at[len(loads)]))
    for copy in kept:
        copy.start()
    for load in both[0]:
        for copy in own(load):
            copy.start()
    for s in range(1, blks):
        top_copy(s).start()
    start(both[1])
    for load in both[1]:
        for copy in own(load):
            copy.start()

    def forward(group):
        def relay(s, carry):
            @pl.when(s > 0)
            def _():
                for load in group:
                    outward(load, s).wait_recv()
                    to_mate(load, s).start()
                    to_across(load, s).start()

            return carry

        def relay_across(s, carry):
            for load in group:
                to_across(load, s).wait_recv()
                passed_on(load, s).start()
            return carry

        def both_ways(s, carry):
            relay(s, carry)
            return relay_across(s - 1, carry)

        lax.fori_loop(1, leaves, both_ways, 0)
        relay_across(leaves - 1, 0)

    def settle(group):
        def one(s, carry):
            for load in group:
                to_mate(load, s).wait_recv()
                passed_on(load, s).wait_recv()
            return carry

        lax.fori_loop(0, leaves, one, 0)

    forward(both[0])
    settle(both[0])
    forward(both[1])
    settle(both[1])
    for copy in kept:
        copy.wait()
    for s in range(1, blks):
        top_copy(s).wait()
    for group in both:
        for load in group:
            for copy in own(load):
                copy.wait_send()

        def drain(s, carry, group=group):
            for load in group:
                outward(load, s).wait_send()
                to_mate(load, s).wait_send()
                to_across(load, s).wait_send()
            return carry

        def drain_last(s, carry, group=group):
            for load in group:
                passed_on(load, s).wait_send()
            return carry

        lax.fori_loop(1, leaves, drain, 0)
        lax.fori_loop(0, leaves, drain_last, 0)


def exchange(heads, tails, codes, top, blk_count):
    leaves = heads.shape[0]
    small = heads.size + tails.size < 4 * 1024 * 1024
    vmem = pl.BlockSpec(memory_space=pltpu.VMEM if small else pl.ANY)
    return pl.pallas_call(
        exchange_kernel,
        out_shape=tuple(
            jax.ShapeDtypeStruct((blk_count,) + x.shape, x.dtype) for x in (heads, tails, codes, top)
        ),
        in_specs=[vmem] * 4,
        out_specs=(vmem,) * 4,
        scratch_shapes=[
            pltpu.SemaphoreType.DMA((3, 4, 2, leaves)),
            pltpu.SemaphoreType.DMA((2, blk_count)),
            pltpu.SemaphoreType.DMA((4,)),
        ],
        compiler_params=pltpu.CompilerParams(collective_id=0, has_side_effects=True),
        name="exchange",
    )(heads, tails, codes, top)


def finish_kernel(me, panel, own, upper, inverse, out):
    per_dest, rows = own.shape[0], own.shape[2]
    blocks = upper.shape[0]
    for k in range(blocks):
        tile = upper[k, me[0]]
        out[0, :, k * rows : (k + 1) * rows] = tile.T
    left = []
    for i in range(per_dest):
        parts = []
        for k in range(blocks):
            parts.append(panel[i + 1, :, k * rows : (k + 1) * rows] - own[i, k])
        left.append(jnp.concatenate(parts, axis=1))
    whole_hi, whole_lo = split(jnp.concatenate(left, axis=0))
    for k in range(blocks):
        wide = (k + 1) * rows
        right = jnp.concatenate([inverse[k, q] for q in range(k + 1)], axis=1)
        right_hi, right_lo = split(right)

        def times(x, y):
            return lax.dot_general(
                x, y, (((1,), (1,)), ((), ())), preferred_element_type=jnp.float32
            )

        solved = (
            times(whole_hi[:, :wide], right_hi)
            + times(whole_lo[:, :wide], right_hi)
            + times(whole_hi[:, :wide], right_lo)
        )
        for i in range(per_dest):
            out[i + 1, :, k * rows : (k + 1) * rows] = solved[i * rows : (i + 1) * rows]


def finish(me, panel, own, upper, inverse):
    smem = pl.BlockSpec(memory_space=pltpu.SMEM)
    vmem = pl.BlockSpec(memory_space=pltpu.VMEM)
    return pl.pallas_call(
        finish_kernel,
        out_shape=jax.ShapeDtypeStruct(panel.shape, panel.dtype),
        in_specs=[smem] + [vmem] * 4,
        out_specs=vmem,
        cost_estimate=pl.CostEstimate(
            flops=6 * panel.size * panel.shape[2], bytes_accessed=8 * panel.size, transcendentals=0
        ),
        name="finish",
    )(me, panel, own, upper, inverse)


def shards(desc_panel, row_map, anc_order, anc_below, anc_panel):
    blk_count = lax.axis_size("blk")
    block_rows = anc_panel.shape[3]
    panel_width = anc_panel.shape[4]
    column_blocks = panel_width // block_rows
    if column_blocks != blk_count or blk_count != 2 * PAIR:
        raise ValueError("unsupported sizes")
    me = lax.axis_index("blk").astype(jnp.int32).reshape(1)
    local_rows = anc_panel.reshape(anc_panel.shape[1], block_rows, panel_width)
    heads, tails, codes = pack(
        row_map, anc_order, anc_below, desc_panel, column_blocks, block_rows
    )
    codes = codes.reshape(codes.shape[0], 1, codes.shape[1])
    heads, tails, codes, top = exchange(heads, tails, codes, local_rows[0], blk_count)
    codes = codes.reshape(-1, codes.shape[-1])
    diag, kept = local_update(me, codes, heads, tails, column_blocks, local_rows.shape[0] - 1)
    upper, inverse = factor(top, diag)
    out = finish(me, local_rows, kept, upper, inverse)
    return out.reshape(anc_panel.shape)


def solution(mesh):
    in_specs = (
        P(("leaf", "blk"), None, None),
        P(("leaf", "blk"), None),
        P(),
        P(),
        P("leaf", None, "blk", None, None),
    )
    out_specs = P("leaf", None, "blk", None, None)
    return jax.shard_map(shards, mesh=mesh, in_specs=in_specs, out_specs=out_specs, check_vma=False)
```

time: 100 us -> 106 us (1.060)
  the two profiles are of different devices: /device:TPU:10 before, /device:TPU:0 now
where the time goes in v3:
time: 106 us; the launch traced here: 105 us
  Pallas kernels  102 us (96%)
  local copies, waits for them, and re-layouts  3.03 us (3%)
    pallas_call x1, Pallas kernels, exchange(): pl.pallas_call(exchange_kernel, out_shape=tuple((jax.ShapeDtypeStruct((bl...  66.1 us
    pallas_call x1, Pallas kernels, factor(): pl.pallas_call(factor_kernel, out_shape=(square, square), in_specs=[pl.Bl...  19.2 us
    pallas_call x1, Pallas kernels, local_update(): pl.pallas_call(update_kernel, grid=(steps,), out_shape=out_shape, in_spec...  10 us
    pallas_call x1, Pallas kernels, finish(): pl.pallas_call(finish_kernel, out_shape=jax.ShapeDtypeStruct(panel.shape,...  4.01 us
    pallas_call x1, Pallas kernels, pack(): pl.pallas_call(pack_kernel, out_shape=(jax.ShapeDtypeStruct((leaves, SLOT...  2.99 us

profile of v3, /device:TPU:0, one launch (start us, length us, event | category | flops | bytes accessed | tf_op | source)
XLA Modules:
  0.0 105.3 jit_solution(5712175029648380647)
XLA Ops:
  0.0 1.3 %copy.6.row_map = s32[8,3]{1,0:T(8,128)} copy(s32[8,3]{0,1:T(4,128)} %param.6) | data formatting | bytes 192 | tf_op args[1]
  1.4 3.0 %pack.1 = (bf16[8,2,128,128]{3,2,1,0:T(8,128)(2,1)}, bf16[8,2,256,128]{3,2,1,0:T(8,128)(2,1)}, s32[8,128]{1,0:T(8,128)}) custom-call(s32[8,3]{1,0:T(8,128)} %copy.6.row_map, s32[8]{0:T(128)} %anc_order.1, s32[8,12]{1,0:T(8,128)} %anc_below.1, bf16[8,384,128]{2,1,0:T(8,128)(2,1)} %panels.1), custom_call_target="tpu_custom_call" | custom-call | tf_op jit(solution)/shard_map/pack/pallas_call | solution.py:171
  4.3 1.7 %slice_bitcast_fusion.top_in = f32[128,512]{1,0:T(8,128)} fusion(f32[1,4,1,128,512]{4,3,2,1,0:T(8,128)} %param.9), kind=kLoop, calls=%fused_computation | loop fusion | bytes 524288 | tf_op jit(solution)/shard_map/squeeze | solution.py:506
  6.0 66.1 %exchange.1 = (bf16[4,8,2,128,128]{4,3,2,1,0:T(8,128)(2,1)}, bf16[4,8,2,256,128]{4,3,2,1,0:T(8,128)(2,1)}, s32[4,8,1,128]{3,2,1,0:T(1,128)}, f32[4,128,512]{2,1,0:T(8,128)}) custom-call(bf16[8,2,128,128]{3,2,1,0:T(8,128)(2,1)} %get-tuple-element.16.heads_in, bf16[8,2,256,128]{3,2,1,0:T(8,128)(2,1)} %get-tuple-element.17.tails_in, s32[8,1,128]{2,1,0:T(1,128)} %bitcast.11, ...), custom_call_target="tpu_custom_call" | custom-call | tf_op jit(solution)/shard_map/exchange/pallas_call | solution.py:429
  72.1 10.0 %update.1 = (f32[4,128,128]{2,1,0:T(8,128)}, f32[3,4,128,128]{3,2,1,0:T(8,128)}) custom-call(s32[1]{0:T(128)} %bitcast.me, s32[32,128]{1,0:T(8,128)} %bitcast.10, bf16[4,8,2,128,128]{4,3,2,1,0:T(8,128)(2,1)} %get-tuple-element.20.heads, bf16[4,8,2,256,128]{4,3,2,1,0:T(8,128)(2,1)} %get-tuple-element.21.tails), custom_call_target="tpu_custom_call" | custom-call | tf_op jit(solution)/shard_map/update/pallas_call | solution.py:240
  82.1 19.2 %factor.1 = (f32[4,4,128,128]{3,2,1,0:T(8,128)}, f32[4,4,128,128]{3,2,1,0:T(8,128)}) custom-call(f32[4,128,512]{2,1,0:T(8,128)} %get-tuple-element.23.top, f32[4,128,128]{2,1,0:T(8,128)} %get-tuple-element.24.own), custom_call_target="tpu_custom_call" | custom-call | flops 268435456 | bytes 67108864 | tf_op jit(solution)/shard_map/factor/pallas_call | solution.py:106
  101.3 4.0 %finish.1 = f32[4,128,512]{2,1,0:T(8,128)} custom-call(s32[1]{0:T(128)} %bitcast.me, f32[4,128,512]{2,1,0:T(8,128)} %bitcast.9, f32[3,4,128,128]{3,2,1,0:T(8,128)} %get-tuple-element.22.own, f32[4,4,128,128]{3,2,1,0:T(8,128)} %get-tuple-element.25.upper, f32[4,4,128,128]{3,2,1,0:T(8,128)} %get-tuple-element.26.inverse), custom_call_target="tpu_custom_call" | custom-call | flops 805306368 | bytes 2097152 | tf_op jit(solution)/shard_map/finish/pallas_call | solution.py:481

commit v4 on v3

--- a/solution.py
+++ b/solution.py
@@ -1,3 +1,5 @@
+import functools
+
 import jax
 import jax.numpy as jnp
 from jax import lax
@@ -58,13 +60,15 @@
                 )
 
 
-def factor_kernel(top, own, upper, inverse, work, strip):
+def factor_kernel(top, own, other, upper, inverse, work, strip):
     blocks, rows = top.shape[0], top.shape[1]
     for j in range(blocks):
         for k in range(blocks):
             tile = top[j, :, k * rows : (k + 1) * rows]
             if j == k:
                 tile = tile - own[k]
+                for n in range(other.shape[0]):
+                    tile = tile - other[n, k]
             work[j, k] = tile
     line = lax.broadcasted_iota(jnp.int32, (rows, rows), 0)
     lane = lax.broadcasted_iota(jnp.int32, (rows, rows), 1)
@@ -100,13 +104,13 @@
     lax.fori_loop(0, blocks, step, 0)
 
 
-def factor(top, own):
+def factor(top, own, other):
     blocks, rows = top.shape[0], top.shape[1]
     square = jax.ShapeDtypeStruct((blocks, blocks, rows, rows), jnp.float32)
     return pl.pallas_call(
         factor_kernel,
         out_shape=(square, square),
-        in_specs=[pl.BlockSpec(memory_space=pltpu.VMEM)] * 2,
+        in_specs=[pl.BlockSpec(memory_space=pltpu.VMEM)] * 3,
         out_specs=(pl.BlockSpec(memory_space=pltpu.VMEM),) * 2,
         scratch_shapes=[
             pltpu.VMEM((blocks, blocks, rows, rows), jnp.float32),
@@ -116,7 +120,7 @@
             flops=2 * (blocks * rows) ** 3, bytes_accessed=64 * 1024 * 1024, transcendentals=0
         ),
         name="factor",
-    )(top, own)
+    )(top, own, other)
 
 
 def pack_kernel(row_map, anc_order, anc_below, panels, heads, tails, codes, count):
@@ -182,77 +186,124 @@
     )(row_map, anc_order, anc_below, panels)
 
 
-def update_kernel(me, codes, heads, tails, diag, kept):
+def times_head(x, head):
+    return lax.dot_general(x, head, (((1,), (1,)), ((), ())), preferred_element_type=jnp.float32)
+
+
+def diag_kernel(position_count, block_count, codes, heads, diag):
+    step = pl.program_id(0)
+    leaves = heads.shape[0]
+
+    @pl.when(step == 0)
+    def _():
+        diag[...] = jnp.zeros_like(diag)
+
+    def absorb(leaf, carry):
+        for slot in range(SLOTS):
+            column = codes[step * leaves + leaf, slot * block_count]
+
+            @pl.when(column < position_count)
+            def _():
+                head = heads[leaf, slot]
+                diag[column] += times_head(head, head)
+
+        return carry
+
+    lax.fori_loop(0, leaves, absorb, 0)
+
+
+def below_kernel(me, codes, heads, tails, kept, sent):
     step = pl.program_id(0)
     leaves = heads.shape[0]
     rows = heads.shape[2]
-    per_dest, columns = kept.shape[0], kept.shape[1]
-    blk_count = columns
+    per_dest = kept.shape[0]
+    half = sent.shape[0] + 1
+    blk_count = half * PAIR
     position_count = (per_dest + 1) * blk_count
     block_count = 1 + tails.shape[2] // rows
 
     @pl.when(step == 0)
     def _():
-        diag[...] = jnp.zeros_like(diag)
         kept[...] = jnp.zeros_like(kept)
-
-    def absorb(s, carry):
-        leaf = lax.div(s, SLOTS)
-        slot = lax.rem(s, SLOTS)
+        sent[...] = jnp.zeros_like(sent)
+
+    def absorb(leaf, carry):
         line = step * leaves + leaf
-        at = slot * block_count
-        column = codes[line, at]
-
-        @pl.when(column < position_count)
-        def _():
-            head = heads[leaf, slot]
-
-            def times(x):
-                return lax.dot_general(
-                    x, head, (((1,), (1,)), ((), ())), preferred_element_type=jnp.float32
-                )
-
-            diag[column] += times(head)
-            for r in range(1, block_count):
-                place = codes[line, at + r]
-                index = lax.div(place, blk_count) - 1
-
-                @pl.when((lax.rem(place, blk_count) == me[0]) & (place < position_count))
-                def _():
-                    kept[index, column] += times(tails[leaf, slot, (r - 1) * rows : r * rows])
-
-        return carry
-
-    lax.fori_loop(0, leaves * SLOTS, absorb, 0)
+        for slot in range(SLOTS):
+            at = slot * block_count
+            column = codes[line, at]
+
+            @pl.when(column < position_count)
+            def _():
+                head = heads[leaf, slot]
+                for r in range(1, block_count):
+                    place = codes[line, at + r]
+                    away = lax.rem(place, blk_count) + blk_count - me[0]
+                    hop = lax.rem(lax.div(away, PAIR), half)
+                    index = lax.div(place, blk_count) - 1
+                    inside = (lax.rem(away, PAIR) == 0) & (place < position_count)
+
+                    def block():
+                        return times_head(tails[leaf, slot, (r - 1) * rows : r * rows], head)
+
+                    @pl.when(inside & (hop == 0))
+                    def _():
+                        kept[index, column] += block()
+
+                    @pl.when(inside & (hop > 0))
+                    def _():
+                        sent[hop - 1, index, column] += block()
+
+        return carry
+
+    lax.fori_loop(0, leaves, absorb, 0)
 
 
 def local_update(me, codes, heads, tails, columns, per_dest):
-    sources, leaves, slots, rows, wide = heads.shape
+    leaves, rows = heads.shape[1], heads.shape[3]
     smem = pl.BlockSpec(memory_space=pltpu.SMEM)
     chunk = min(leaves, 8)
-    steps = sources * leaves // chunk
+    steps = heads.shape[0] * leaves // chunk
+    block_count = 1 + tails.shape[3] // rows
     heads = heads.reshape((steps, chunk) + heads.shape[2:])
     tails = tails.reshape((steps, chunk) + tails.shape[2:])
-    out_shape = (
-        jax.ShapeDtypeStruct((columns, rows, rows), jnp.float32),
-        jax.ShapeDtypeStruct((per_dest, columns, rows, rows), jnp.float32),
+
+    def streamed(x):
+        return pl.BlockSpec((None,) + x.shape[1:], lambda i: (i, 0, 0, 0, 0))
+
+    def held(x):
+        return pl.BlockSpec(x.shape, lambda i: (0,) * len(x.shape))
+
+    def cost(x):
+        return pl.CostEstimate(
+            flops=2 * x.size * rows, bytes_accessed=8 * x.size, transcendentals=0
+        )
+
+    diag_shape = jax.ShapeDtypeStruct((columns, rows, rows), jnp.float32)
+    diag = pl.pallas_call(
+        functools.partial(diag_kernel, (per_dest + 1) * columns, block_count),
+        grid=(steps,),
+        out_shape=diag_shape,
+        in_specs=[smem, streamed(heads)],
+        out_specs=held(diag_shape),
+        cost_estimate=cost(heads),
+        name="diag_update",
+    )(codes, heads)
+    tiles = (per_dest, columns, rows, rows)
+    below_shape = (
+        jax.ShapeDtypeStruct(tiles, jnp.float32),
+        jax.ShapeDtypeStruct((columns // PAIR - 1,) + tiles, jnp.float32),
     )
-    return pl.pallas_call(
-        update_kernel,
+    kept, sent = pl.pallas_call(
+        below_kernel,
         grid=(steps,),
-        out_shape=out_shape,
-        in_specs=[
-            smem,
-            smem,
-            pl.BlockSpec((None,) + heads.shape[1:], lambda i: (i, 0, 0, 0, 0)),
-            pl.BlockSpec((None,) + tails.shape[1:], lambda i: (i, 0, 0, 0, 0)),
-        ],
-        out_specs=(
-            pl.BlockSpec(out_shape[0].shape, lambda i: (0, 0, 0)),
-            pl.BlockSpec(out_shape[1].shape, lambda i: (0, 0, 0, 0)),
-        ),
-        name="update",
+        out_shape=below_shape,
+        in_specs=[smem, smem, streamed(heads), streamed(tails)],
+        out_specs=tuple(held(x) for x in below_shape),
+        cost_estimate=cost(tails),
+        name="below_update",
     )(me, codes, heads, tails)
+    return diag, kept, sent
 
 
 def exchange_kernel(
@@ -263,7 +314,6 @@
     leaf = lax.axis_index("leaf")
     blk = lax.axis_index("blk")
     mate = blk + 1 - 2 * lax.rem(blk, PAIR)
-    across = lax.rem(blk + PAIR, blks)
     MESH = pl.DeviceIdType.MESH
     loads = ((codes_in, codes), (heads_in, heads), (tails_in, tails))
 
@@ -307,24 +357,13 @@
         held = loads[load][1]
         return remote(held.at[0, came(s)], held.at[1, came(s)], load, 1, s, leaf, mate)
 
-    def to_across(load, s):
-        held = loads[load][1]
-        return remote(held.at[0, came(s)], held.at[2, came(s)], load, 2, s, leaf, across)
-
-    def passed_on(load, s):
-        held = loads[load][1]
-        return remote(held.at[2, came(s)], held.at[3, came(s)], load, 3, s, leaf, mate)
-
     def own(load):
         source, held = loads[load]
-        return (
-            remote(source.at[leaf], held.at[1, leaf], load, 1, 0, leaf, mate),
-            remote(source.at[leaf], held.at[2, leaf], load, 2, 0, leaf, across),
-        )
+        return (remote(source.at[leaf], held.at[1, leaf], load, 1, 0, leaf, mate),)
 
     def top_copy(s):
         return pltpu.make_async_remote_copy(
-            src_ref=top_in,
+            src_ref=top_in.at[0],
             dst_ref=tops.at[blk],
             send_sem=top_sems.at[0, s],
             recv_sem=top_sems.at[1, s],
@@ -347,7 +386,7 @@
         pltpu.make_async_copy(source.at[leaf], held.at[0, leaf], local.at[load])
         for load, (source, held) in enumerate(loads)
     ]
-    kept.append(pltpu.make_async_copy(top_in, tops.at[blk], local.at[len(loads)]))
+    kept.append(pltpu.make_async_copy(top_in.at[0], tops.at[blk], local.at[len(loads)]))
     for copy in kept:
         copy.start()
     for load in both[0]:
@@ -361,42 +400,16 @@
             copy.start()
 
     def forward(group):
-        def relay(s, carry):
-            @pl.when(s > 0)
-            def _():
-                for load in group:
-                    outward(load, s).wait_recv()
-                    to_mate(load, s).start()
-                    to_across(load, s).start()
-
-            return carry
-
-        def relay_across(s, carry):
-            for load in group:
-                to_across(load, s).wait_recv()
-                passed_on(load, s).start()
-            return carry
-
-        def both_ways(s, carry):
-            relay(s, carry)
-            return relay_across(s - 1, carry)
-
-        lax.fori_loop(1, leaves, both_ways, 0)
-        relay_across(leaves - 1, 0)
-
-    def settle(group):
         def one(s, carry):
             for load in group:
-                to_mate(load, s).wait_recv()
-                passed_on(load, s).wait_recv()
+                outward(load, s).wait_recv()
+                to_mate(load, s).start()
             return carry
 
-        lax.fori_loop(0, leaves, one, 0)
-
-    forward(both[0])
-    settle(both[0])
-    forward(both[1])
-    settle(both[1])
+        lax.fori_loop(1, leaves, one, 0)
+
+    for group in both:
+        forward(group)
     for copy in kept:
         copy.wait()
     for s in range(1, blks):
@@ -404,46 +417,41 @@
     for group in both:
         for load in group:
             for copy in own(load):
-                copy.wait_send()
+                copy.wait()
 
         def drain(s, carry, group=group):
             for load in group:
                 outward(load, s).wait_send()
-                to_mate(load, s).wait_send()
-                to_across(load, s).wait_send()
+                to_mate(load, s).wait()
             return carry
 
-        def drain_last(s, carry, group=group):
-            for load in group:
-                passed_on(load, s).wait_send()
-            return carry
-
         lax.fori_loop(1, leaves, drain, 0)
-        lax.fori_loop(0, leaves, drain_last, 0)
-
-
-def exchange(heads, tails, codes, top, blk_count):
+
+
+def exchange(heads, tails, codes, panel, blk_count):
     leaves = heads.shape[0]
     small = heads.size + tails.size < 4 * 1024 * 1024
     vmem = pl.BlockSpec(memory_space=pltpu.VMEM if small else pl.ANY)
     return pl.pallas_call(
         exchange_kernel,
         out_shape=tuple(
-            jax.ShapeDtypeStruct((blk_count,) + x.shape, x.dtype) for x in (heads, tails, codes, top)
-        ),
+            jax.ShapeDtypeStruct((count,) + x.shape, x.dtype)
+            for count, x in ((PAIR, heads), (PAIR, tails), (PAIR, codes))
+        )
+        + (jax.ShapeDtypeStruct((blk_count,) + panel.shape[1:], panel.dtype),),
         in_specs=[vmem] * 4,
         out_specs=(vmem,) * 4,
         scratch_shapes=[
-            pltpu.SemaphoreType.DMA((3, 4, 2, leaves)),
+            pltpu.SemaphoreType.DMA((3, 2, 2, leaves)),
             pltpu.SemaphoreType.DMA((2, blk_count)),
             pltpu.SemaphoreType.DMA((4,)),
         ],
         compiler_params=pltpu.CompilerParams(collective_id=0, has_side_effects=True),
         name="exchange",
-    )(heads, tails, codes, top)
-
-
-def finish_kernel(me, panel, own, upper, inverse, out):
+    )(heads, tails, codes, panel)
+
+
+def finish_kernel(me, panel, own, other, upper, inverse, out):
     per_dest, rows = own.shape[0], own.shape[2]
     blocks = upper.shape[0]
     for k in range(blocks):
@@ -453,7 +461,10 @@
     for i in range(per_dest):
         parts = []
         for k in range(blocks):
-            parts.append(panel[i + 1, :, k * rows : (k + 1) * rows] - own[i, k])
+            tile = panel[i + 1, :, k * rows : (k + 1) * rows] - own[i, k]
+            for n in range(other.shape[0]):
+                tile = tile - other[n, i, k]
+            parts.append(tile)
         left.append(jnp.concatenate(parts, axis=1))
     whole_hi, whole_lo = split(jnp.concatenate(left, axis=0))
     for k in range(blocks):
@@ -475,19 +486,19 @@
             out[i + 1, :, k * rows : (k + 1) * rows] = solved[i * rows : (i + 1) * rows]
 
 
-def finish(me, panel, own, upper, inverse):
+def finish(me, panel, own, other, upper, inverse):
     smem = pl.BlockSpec(memory_space=pltpu.SMEM)
     vmem = pl.BlockSpec(memory_space=pltpu.VMEM)
     return pl.pallas_call(
         finish_kernel,
         out_shape=jax.ShapeDtypeStruct(panel.shape, panel.dtype),
-        in_specs=[smem] + [vmem] * 4,
+        in_specs=[smem] + [vmem] * 5,
         out_specs=vmem,
         cost_estimate=pl.CostEstimate(
             flops=6 * panel.size * panel.shape[2], bytes_accessed=8 * panel.size, transcendentals=0
         ),
         name="finish",
-    )(me, panel, own, upper, inverse)
+    )(me, panel, own, other, upper, inverse)
 
 
 def shards(desc_panel, row_map, anc_order, anc_below, anc_panel):
@@ -503,11 +514,19 @@
         row_map, anc_order, anc_below, desc_panel, column_blocks, block_rows
     )
     codes = codes.reshape(codes.shape[0], 1, codes.shape[1])
-    heads, tails, codes, top = exchange(heads, tails, codes, local_rows[0], blk_count)
+    heads, tails, codes, top = exchange(heads, tails, codes, local_rows, blk_count)
     codes = codes.reshape(-1, codes.shape[-1])
-    diag, kept = local_update(me, codes, heads, tails, column_blocks, local_rows.shape[0] - 1)
-    upper, inverse = factor(top, diag)
-    out = finish(me, local_rows, kept, upper, inverse)
+    diag, kept, sent = local_update(me, codes, heads, tails, column_blocks, local_rows.shape[0] - 1)
+
+    def shift(x, by):
+        return lax.ppermute(x, "blk", [(b, (b + by) % blk_count) for b in range(blk_count)])
+
+    hops = range(1, blk_count // PAIR)
+    other_diag = jnp.stack([shift(diag, PAIR * s) for s in hops])
+    other_diag, sent = lax.optimization_barrier((other_diag, sent))
+    other_below = jnp.stack([shift(sent[s - 1], PAIR * s) for s in hops])
+    upper, inverse = factor(top, diag, other_diag)
+    out = finish(me, local_rows, kept, other_below, upper, inverse)
     return out.reshape(anc_panel.shape)
 
 

time: 106 us -> 87.7 us (0.83)
  the two profiles are of different devices: /device:TPU:0 before, /device:TPU:26 now
where the time goes in v4:
time: 87.7 us; the launch traced here: 88 us
  Pallas kernels  81 us (92%)
  starting transfers between devices  3.54 us (4%)
  local copies, waits for them, and re-layouts  2.22 us (3%)
  waiting for transfers between devices  1.19 us (1%)
    pallas_call x1, Pallas kernels, exchange(): pl.pallas_call(exchange_kernel, out_shape=tuple((jax.ShapeDtypeStruct((co...  44 us
    pallas_call x1, Pallas kernels, factor(): pl.pallas_call(factor_kernel, out_shape=(square, square), in_specs=[pl.Bl...  19.3 us
    pallas_call x1, Pallas kernels, local_update(): pl.pallas_call(below_kernel, grid=(steps,), out_shape=below_shape, in_spe...  5.86 us
    pallas_call x1, Pallas kernels, local_update(): pl.pallas_call(functools.partial(diag_kernel, (per_dest + 1) * columns, b...  4.62 us
    pallas_call x1, Pallas kernels, finish(): pl.pallas_call(finish_kernel, out_shape=jax.ShapeDtypeStruct(panel.shape,...  4.24 us
    ppermute x2, starting transfers between devices, shift(): lax.ppermute(x, 'blk', [(b, (b + by) % blk_count) for b in range(blk_coun...  3.54 us
    pallas_call x1, Pallas kernels, pack(): pl.pallas_call(pack_kernel, out_shape=(jax.ShapeDtypeStruct((leaves, SLOT...  2.99 us
    unnamed x5, local copies, waits for them, and re-layouts  2.22 us
  transfers between devices with their start and end apart: 2, of which 1 were waited for; matrix products, arithmetic and copies ran while one was open for 0% of the time, Pallas kernels for 29%

profile of v4, /device:TPU:26, one launch (start us, length us, event | category | flops | bytes accessed | tf_op | source)
XLA Modules:
  0.0 88.0 jit_solution(13368902754468615298)
XLA Ops:
  0.0 1.3 %copy.6.row_map = s32[8,3]{1,0:T(8,128)} copy(s32[8,3]{0,1:T(4,128)} %param.6) | data formatting | bytes 192 | tf_op args[1]
  1.3 3.0 %pack.1 = (bf16[8,2,128,128]{3,2,1,0:T(8,128)(2,1)}, bf16[8,2,256,128]{3,2,1,0:T(8,128)(2,1)}, s32[8,128]{1,0:T(8,128)}) custom-call(s32[8,3]{1,0:T(8,128)} %copy.6.row_map, s32[8]{0:T(128)} %anc_order.1, s32[8,12]{1,0:T(8,128)} %anc_below.1, bf16[8,384,128]{2,1,0:T(8,128)(2,1)} %panels.1), custom_call_target="tpu_custom_call" | custom-call | tf_op jit(solution)/shard_map/pack/pallas_call | solution.py:175
  4.3 44.0 %exchange.1 = (bf16[2,8,2,128,128]{4,3,2,1,0:T(8,128)(2,1)}, bf16[2,8,2,256,128]{4,3,2,1,0:T(8,128)(2,1)}, s32[2,8,1,128]{3,2,1,0:T(1,128)}, f32[4,128,512]{2,1,0:T(8,128)}) custom-call(bf16[8,2,128,128]{3,2,1,0:T(8,128)(2,1)} %get-tuple-element.18.heads_in, bf16[8,2,256,128]{3,2,1,0:T(8,128)(2,1)} %get-tuple-element.19.tails_in, s32[8,1,128]{2,1,0:T(1,128)} %bitcast.16, ...), custom_call_target="tpu_custom_call" | custom-call | tf_op jit(solution)/shard_map/exchange/pallas_call | solution.py:435
  48.4 4.6 %diag_update.1.own = f32[4,128,128]{2,1,0:T(8,128)} custom-call(s32[16,128]{1,0:T(8,128)} %bitcast.14, bf16[2,8,2,128,128]{4,3,2,1,0:T(8,128)(2,1)} %get-tuple-element.22.heads), custom_call_target="tpu_custom_call" | custom-call | flops 134217728 | bytes 4194304 | tf_op jit(solution)/shard_map/diag_update/pallas_call | solution.py:283
  53.0 1.8 %collective-permute-start = (f32[4,128,128]{2,1,0:T(8,128)}, f32[4,128,128]{2,1,0:T(8,128)S(1)}, u32[]{:S(2)}, u32[]{:S(2)}) collective-permute-start(f32[4,128,128]{2,1,0:T(8,128)} %diag_update.1.own), channel_id=1, source_target_pairs={{0,2},{1,3},{2,0},{3,1},{4,6},{5,7},{6,4},{7,5},{8,10},{9,11},{10,... | collective-permute-start | bytes 786440 | tf_op jit(solution)/shard_map/ppermute | solution.py:522
  54.8 5.9 %below_update.1 = (f32[3,4,128,128]{3,2,1,0:T(8,128)}, f32[1,3,4,128,128]{4,3,2,1,0:T(8,128)}) custom-call(s32[1]{0:T(128)} %bitcast.me, s32[16,128]{1,0:T(8,128)} %bitcast.15, bf16[2,8,2,128,128]{4,3,2,1,0:T(8,128)(2,1)} %get-tuple-element.22.heads, bf16[2,8,2,256,128]{4,3,2,1,0:T(8,128)(2,1)} %get-tuple-element.23.tails), custom_call_target="tpu_custom_call" | custom-call | flops 268435456 | bytes 8388608 | tf_op jit(solution)/shard_map/below_update/pallas_call | solution.py:297
  60.7 1.2 %collective-permute-done = f32[4,128,128]{2,1,0:T(8,128)S(1)} collective-permute-done((f32[4,128,128]{2,1,0:T(8,128)}, f32[4,128,128]{2,1,0:T(8,128)S(1)}, u32[]{:S(2)}, u32[]{:S(2)}) %collective-permute-start) | collective-permute-done | bytes 262176 | tf_op jit(solution)/shard_map/ppermute | solution.py:522
  61.8 0.0 copy-start.1
  61.8 1.7 %collective-permute-start.1 = (f32[3,4,128,128]{3,2,1,0:T(8,128)}, f32[3,4,128,128]{3,2,1,0:T(8,128)S(1)}, u32[]{:S(2)}, u32[]{:S(2)}) collective-permute-start(f32[3,4,128,128]{3,2,1,0:T(8,128)} %bitcast.17), channel_id=1, source_target_pairs={{0,2},{1,3},{2,0},{3,1},{4,6},{5,7},{6,4},{7,5},{8,10},{9,11},{10,... | collective-permute-start | bytes 2359304 | tf_op jit(solution)/shard_map/ppermute | solution.py:522
  63.6 0.0 copy-done.1
  63.6 19.3 %factor.1 = (f32[4,4,128,128]{3,2,1,0:T(8,128)}, f32[4,4,128,128]{3,2,1,0:T(8,128)}) custom-call(f32[4,128,512]{2,1,0:T(8,128)} %get-tuple-element.27.top, f32[4,128,128]{2,1,0:T(8,128)} %diag_update.1.own, f32[1,4,128,128]{3,2,1,0:T(8,128)} %bitcast.13), custom_call_target="tpu_custom_call" | custom-call | flops 268435456 | bytes 67108864 | tf_op jit(solution)/shard_map/factor/pallas_call | solution.py:110
  82.9 0.0 collective-permute-done.1
  82.9 0.0 copy-start
  82.9 0.9 copy-done
  83.8 4.2 %finish.1 = f32[4,128,512]{2,1,0:T(8,128)} custom-call(s32[1]{0:T(128)} %bitcast.me, f32[4,128,512]{2,1,0:T(8,128)} %bitcast.11, f32[3,4,128,128]{3,2,1,0:T(8,128)} %get-tuple-element.24.own, f32[1,3,4,128,128]{4,3,2,1,0:T(8,128)} %bitcast.12, f32[4,4,128,128]{3,2,1,0:T(8,128)} %get-tuple-element.29.upper, f32[4,4,128,128]{3,2,1,0:T(8,128)} %get-tuple-element.30.inverse), custom_call_target="tpu_custom_call" | custom-call | flops 805306368 | bytes 2097152 | tf_op jit(solution)/shard_map/finish/pallas_call | solution.py:492
Async XLA Ops:
  53.0 8.8 %collective-permute-start = (f32[4,128,128]{2,1,0:T(8,128)}, f32[4,128,128]{2,1,0:T(8,128)S(1)}, u32[]{:S(2)}, u32[]{:S(2)}) collective-permute-start(f32[4,128,128]{2,1,0:T(8,128)} %diag_update.1.own), channel_id=1, source_target_pairs={{0,2},{1,3},{2,0},{3,1},{4,6},{5,7},{6,4},{7,5},{8,10},{9,11},{10,... | collective-permute-start | bytes 786440 | tf_op jit(solution)/shard_map/ppermute | solution.py:522
  61.8 1.7 %copy-start.1 = (f32[4,128,128]{2,1,0:T(8,128)}, f32[4,128,128]{2,1,0:T(8,128)S(1)}, u32[]{:S(2)}) copy-start(f32[4,128,128]{2,1,0:T(8,128)S(1)} %collective-permute-done) | copy-start | bytes 786436
  61.8 21.0 %collective-permute-start.1 = (f32[3,4,128,128]{3,2,1,0:T(8,128)}, f32[3,4,128,128]{3,2,1,0:T(8,128)S(1)}, u32[]{:S(2)}, u32[]{:S(2)}) collective-permute-start(f32[3,4,128,128]{3,2,1,0:T(8,128)} %bitcast.17), channel_id=1, source_target_pairs={{0,2},{1,3},{2,0},{3,1},{4,6},{5,7},{6,4},{7,5},{8,10},{9,11},{10,... | collective-permute-start | bytes 2359304 | tf_op jit(solution)/shard_map/ppermute | solution.py:522
  82.9 0.9 copy-start

commit v5 on v4

--- a/solution.py
+++ b/solution.py
@@ -371,7 +371,7 @@
             device_id_type=MESH,
         )
 
-    both = ((0, 1), (2,))
+    both = ((0, 1, 2), ())
 
     def start(group):
         def one(s, carry):

time: 87.7 us -> 88.2 us (level); the launches traced: 88 us -> 86.5 us
  Pallas kernels: 81 us -> 78.9 us
  waiting for transfers between devices: 1.19 us -> 2.87 us
  starting transfers between devices: 3.54 us -> 2.47 us
    ppermute x2, waiting for transfers between devices: 1.19 us -> 2.87 us  [shift(): lax.ppermute(x, 'blk', [(b, (b + by) % blk_count) for b in range(blk_coun...]
    pallas_call x1, Pallas kernels: 5.86 us -> 4.69 us  [local_update(): pl.pallas_call(below_kernel, grid=(steps,), out_shape=below_shape, in_spe...]
    pallas_call x1, Pallas kernels: 4.62 us -> 3.51 us  [local_update(): pl.pallas_call(functools.partial(diag_kernel, (per_dest + 1) * columns, b...]
    ppermute x2, starting transfers between devices: 3.54 us -> 2.47 us  [shift(): lax.ppermute(x, 'blk', [(b, (b + by) % blk_count) for b in range(blk_coun...]
  transfers between devices with their start and end apart: 2 -> 2, of which waited for: 1 -> 1; matrix products, arithmetic and copies ran while one was open for 0% -> 0% of each run, Pallas kernels for 29% -> 28%
where the time goes in v5:
time: 88.2 us; the launch traced here: 86.5 us
  Pallas kernels  78.9 us (89%)
  waiting for transfers between devices  2.87 us (3%)
  starting transfers between devices  2.47 us (3%)
  local copies, waits for them, and re-layouts  2.22 us (3%)
    pallas_call x1, Pallas kernels, exchange(): pl.pallas_call(exchange_kernel, out_shape=tuple((jax.ShapeDtypeStruct((co...  44.2 us
    pallas_call x1, Pallas kernels, factor(): pl.pallas_call(factor_kernel, out_shape=(square, square), in_specs=[pl.Bl...  19.3 us
    pallas_call x1, Pallas kernels, local_update(): pl.pallas_call(below_kernel, grid=(steps,), out_shape=below_shape, in_spe...  4.69 us
    pallas_call x1, Pallas kernels, finish(): pl.pallas_call(finish_kernel, out_shape=jax.ShapeDtypeStruct(panel.shape,...  4.24 us
    pallas_call x1, Pallas kernels, local_update(): pl.pallas_call(functools.partial(diag_kernel, (per_dest + 1) * columns, b...  3.51 us
    pallas_call x1, Pallas kernels, pack(): pl.pallas_call(pack_kernel, out_shape=(jax.ShapeDtypeStruct((leaves, SLOT...  2.99 us
    ppermute x2, waiting for transfers between devices, shift(): lax.ppermute(x, 'blk', [(b, (b + by) % blk_count) for b in range(blk_coun...  2.87 us
    ppermute x2, starting transfers between devices, shift(): lax.ppermute(x, 'blk', [(b, (b + by) % blk_count) for b in range(blk_coun...  2.47 us
  transfers between devices with their start and end apart: 2, of which 1 were waited for; matrix products, arithmetic and copies ran while one was open for 0% of the time, Pallas kernels for 28%

profile of v5, /device:TPU:26, one launch (start us, length us, event | category | flops | bytes accessed | tf_op | source)
XLA Modules:
  0.0 86.5 jit_solution(17378842524493586330)
XLA Ops:
  0.0 1.3 %copy.6.row_map = s32[8,3]{1,0:T(8,128)} copy(s32[8,3]{0,1:T(4,128)} %param.6) | data formatting | bytes 192 | tf_op args[1]
  1.3 3.0 %pack.1 = (bf16[8,2,128,128]{3,2,1,0:T(8,128)(2,1)}, bf16[8,2,256,128]{3,2,1,0:T(8,128)(2,1)}, s32[8,128]{1,0:T(8,128)}) custom-call(s32[8,3]{1,0:T(8,128)} %copy.6.row_map, s32[8]{0:T(128)} %anc_order.1, s32[8,12]{1,0:T(8,128)} %anc_below.1, bf16[8,384,128]{2,1,0:T(8,128)(2,1)} %panels.1), custom_call_target="tpu_custom_call" | custom-call | tf_op jit(solution)/shard_map/pack/pallas_call | solution.py:175
  4.3 44.2 %exchange.1 = (bf16[2,8,2,128,128]{4,3,2,1,0:T(8,128)(2,1)}, bf16[2,8,2,256,128]{4,3,2,1,0:T(8,128)(2,1)}, s32[2,8,1,128]{3,2,1,0:T(1,128)}, f32[4,128,512]{2,1,0:T(8,128)}) custom-call(bf16[8,2,128,128]{3,2,1,0:T(8,128)(2,1)} %get-tuple-element.18.heads_in, bf16[8,2,256,128]{3,2,1,0:T(8,128)(2,1)} %get-tuple-element.19.tails_in, s32[8,1,128]{2,1,0:T(1,128)} %bitcast.16, ...), custom_call_target="tpu_custom_call" | custom-call | tf_op jit(solution)/shard_map/exchange/pallas_call | solution.py:435
  48.6 3.5 %diag_update.1.own = f32[4,128,128]{2,1,0:T(8,128)} custom-call(s32[16,128]{1,0:T(8,128)} %bitcast.14, bf16[2,8,2,128,128]{4,3,2,1,0:T(8,128)(2,1)} %get-tuple-element.22.heads), custom_call_target="tpu_custom_call" | custom-call | flops 134217728 | bytes 4194304 | tf_op jit(solution)/shard_map/diag_update/pallas_call | solution.py:283
  52.1 1.2 %collective-permute-start = (f32[4,128,128]{2,1,0:T(8,128)}, f32[4,128,128]{2,1,0:T(8,128)S(1)}, u32[]{:S(2)}, u32[]{:S(2)}) collective-permute-start(f32[4,128,128]{2,1,0:T(8,128)} %diag_update.1.own), channel_id=1, source_target_pairs={{0,2},{1,3},{2,0},{3,1},{4,6},{5,7},{6,4},{7,5},{8,10},{9,11},{10,... | collective-permute-start | bytes 786440 | tf_op jit(solution)/shard_map/ppermute | solution.py:522
  53.3 4.7 %below_update.1 = (f32[3,4,128,128]{3,2,1,0:T(8,128)}, f32[1,3,4,128,128]{4,3,2,1,0:T(8,128)}) custom-call(s32[1]{0:T(128)} %bitcast.me, s32[16,128]{1,0:T(8,128)} %bitcast.15, bf16[2,8,2,128,128]{4,3,2,1,0:T(8,128)(2,1)} %get-tuple-element.22.heads, bf16[2,8,2,256,128]{4,3,2,1,0:T(8,128)(2,1)} %get-tuple-element.23.tails), custom_call_target="tpu_custom_call" | custom-call | flops 268435456 | bytes 8388608 | tf_op jit(solution)/shard_map/below_update/pallas_call | solution.py:297
  58.0 2.9 %collective-permute-done = f32[4,128,128]{2,1,0:T(8,128)S(1)} collective-permute-done((f32[4,128,128]{2,1,0:T(8,128)}, f32[4,128,128]{2,1,0:T(8,128)S(1)}, u32[]{:S(2)}, u32[]{:S(2)}) %collective-permute-start) | collective-permute-done | bytes 262176 | tf_op jit(solution)/shard_map/ppermute | solution.py:522
  60.9 0.0 copy-start.1
  60.9 1.2 %collective-permute-start.1 = (f32[3,4,128,128]{3,2,1,0:T(8,128)}, f32[3,4,128,128]{3,2,1,0:T(8,128)S(1)}, u32[]{:S(2)}, u32[]{:S(2)}) collective-permute-start(f32[3,4,128,128]{3,2,1,0:T(8,128)} %bitcast.17), channel_id=1, source_target_pairs={{0,2},{1,3},{2,0},{3,1},{4,6},{5,7},{6,4},{7,5},{8,10},{9,11},{10,... | collective-permute-start | bytes 2359304 | tf_op jit(solution)/shard_map/ppermute | solution.py:522
  62.1 0.0 copy-done.1
  62.1 19.3 %factor.1 = (f32[4,4,128,128]{3,2,1,0:T(8,128)}, f32[4,4,128,128]{3,2,1,0:T(8,128)}) custom-call(f32[4,128,512]{2,1,0:T(8,128)} %get-tuple-element.27.top, f32[4,128,128]{2,1,0:T(8,128)} %diag_update.1.own, f32[1,4,128,128]{3,2,1,0:T(8,128)} %bitcast.13), custom_call_target="tpu_custom_call" | custom-call | flops 268435456 | bytes 67108864 | tf_op jit(solution)/shard_map/factor/pallas_call | solution.py:110
  81.4 0.0 collective-permute-done.1
  81.4 0.0 copy-start
  81.4 0.9 %copy-done = f32[3,4,128,128]{3,2,1,0:T(8,128)} copy-done((f32[3,4,128,128]{3,2,1,0:T(8,128)}, f32[3,4,128,128]{3,2,1,0:T(8,128)S(1)}, u32[]{:S(2)}) %copy-start) | copy-done | bytes 786456
  82.3 4.2 %finish.1 = f32[4,128,512]{2,1,0:T(8,128)} custom-call(s32[1]{0:T(128)} %bitcast.me, f32[4,128,512]{2,1,0:T(8,128)} %bitcast.11, f32[3,4,128,128]{3,2,1,0:T(8,128)} %get-tuple-element.24.own, f32[1,3,4,128,128]{4,3,2,1,0:T(8,128)} %bitcast.12, f32[4,4,128,128]{3,2,1,0:T(8,128)} %get-tuple-element.29.upper, f32[4,4,128,128]{3,2,1,0:T(8,128)} %get-tuple-element.30.inverse), custom_call_target="tpu_custom_call" | custom-call | flops 805306368 | bytes 2097152 | tf_op jit(solution)/shard_map/finish/pallas_call | solution.py:492
Async XLA Ops:
  52.1 8.8 %collective-permute-start = (f32[4,128,128]{2,1,0:T(8,128)}, f32[4,128,128]{2,1,0:T(8,128)S(1)}, u32[]{:S(2)}, u32[]{:S(2)}) collective-permute-start(f32[4,128,128]{2,1,0:T(8,128)} %diag_update.1.own), channel_id=1, source_target_pairs={{0,2},{1,3},{2,0},{3,1},{4,6},{5,7},{6,4},{7,5},{8,10},{9,11},{10,... | collective-permute-start | bytes 786440 | tf_op jit(solution)/shard_map/ppermute | solution.py:522
  60.9 1.2 %copy-start.1 = (f32[4,128,128]{2,1,0:T(8,128)}, f32[4,128,128]{2,1,0:T(8,128)S(1)}, u32[]{:S(2)}) copy-start(f32[4,128,128]{2,1,0:T(8,128)S(1)} %collective-permute-done) | copy-start | bytes 786436
  60.9 20.5 %collective-permute-start.1 = (f32[3,4,128,128]{3,2,1,0:T(8,128)}, f32[3,4,128,128]{3,2,1,0:T(8,128)S(1)}, u32[]{:S(2)}, u32[]{:S(2)}) collective-permute-start(f32[3,4,128,128]{3,2,1,0:T(8,128)} %bitcast.17), channel_id=1, source_target_pairs={{0,2},{1,3},{2,0},{3,1},{4,6},{5,7},{6,4},{7,5},{8,10},{9,11},{10,... | collective-permute-start | bytes 2359304 | tf_op jit(solution)/shard_map/ppermute | solution.py:522
  81.4 0.9 %copy-start = (f32[3,4,128,128]{3,2,1,0:T(8,128)}, f32[3,4,128,128]{3,2,1,0:T(8,128)S(1)}, u32[]{:S(2)}) copy-start(f32[3,4,128,128]{3,2,1,0:T(8,128)S(1)} %collective-permute-done.1) | copy-start | bytes 2359300
